TPU v7x, 32 devices: a whole 2x2x4 slice. The times are simulated.
32 devices in a mesh: row: 16 (over z, y, x), col: 2 (over core).
Axes of the slice: x: 2, y: 2, z: 4, core: 2. Of those that a mesh axis runs over, the one named last changes fastest.
Arguments:
- messages: float32 [32, 16, 2, 16, 128], P(('row', 'col')), may hold values from -6 to 6
- dst_local: int32 [32, 16, 2, 16], P(('row', 'col')), may hold values from 0 to 255
- counts: int32 [32, 16, 2], P(('row', 'col')), may hold values from 8 to 16, as said below
- degrees: int32 [8192], P(('row', 'col')), may hold values from 1 to 8
Outputs:
- aggregate: float32 [8192, 128], P(('row', 'col'))
Inputs may be any that keep to these rules, and one draw needn't show every extreme that they name: For every sender and group, the counts over the group's 2 ranges sum to exactly 24. In each group one range receives 16 live slots from every sender.
All inputs are finite; a program needn't handle non-finite values.
Results may differ from a plain program's by a relative error of at most 0.0003.
Values sent between devices are 32-bit elements; how exact they have to be, the bound alone decides.
No kernel may reach another device: no remote copies, remote signals or barrier semaphores. Data moves between devices by JAX's collectives and lax.ppermute only.
A program may use at most 64 MiB of HBM per device.

v0:
```python
import jax
import jax.numpy as jnp
from jax import lax
from jax.sharding import PartitionSpec as P


def body(messages, dst_local, counts, degrees):
    slots = messages.shape[3]
    width = messages.shape[4]
    owned = degrees.shape[0]
    slot_index = lax.broadcasted_iota(jnp.int32, counts.shape + (slots,), 3)
    alive_int = (slot_index < counts[..., None]).astype(jnp.int32)
    alive_mask = alive_int.astype(jnp.float32)
    masked = messages * alive_mask[..., None]
    received, labels = (
        lax.all_to_all(
            lax.all_to_all(masked, "row", split_axis=1, concat_axis=0, tiled=True),
            "col",
            split_axis=2,
            concat_axis=1,
            tiled=True,
        ),
        lax.all_to_all(
            lax.all_to_all(dst_local, "row", split_axis=1, concat_axis=0, tiled=True),
            "col",
            split_axis=2,
            concat_axis=1,
            tiled=True,
        ),
    )
    summed = jax.ops.segment_sum(
        received.reshape(-1, width), labels.reshape(-1), num_segments=owned
    )
    scale = jnp.maximum(degrees, 1).astype(jnp.float32)
    return summed / scale[:, None]


def solution(mesh):
    in_specs = (
        P(("row", "col"), None, None, None, None),
        P(("row", "col"), None, None, None),
        P(("row", "col"), None, None),
        P(("row", "col")),
    )
    out_specs = P(("row", "col"), None)
    return jax.shard_map(body, mesh=mesh, in_specs=in_specs, out_specs=out_specs, check_vma=False)
```

profile of v0, /device:TPU:0, one launch (start us, length us, event | category | flops | bytes accessed | tf_op | source)
XLA Modules:
  0.0 40.6 jit_solution(9112248974094976545)
XLA Ops:
  0.0 8.3 %all-to-all-start = ((s32[1,16,2,16]{3,2,0,1:T(2,128)}), s32[1,16,2,16]{3,2,0,1:T(2,128)S(1)}, u32[]{:S(2)}, u32[]{:S(2)}) async-start(s32[1,16,2,16]{3,2,0,1:T(2,128)} %bitcast.18), calls=%async_computation | async-start | bytes 32768 | tf_op jit(solution)/shard_map/all_to_all | solution.py:24
  8.3 0.0 copy-start
  8.4 0.7 %copy-done = s32[1,16,2]{1,2,0:T(2,128)S(1)} copy-done((s32[1,16,2]{1,2,0:T(2,128)S(1)}, s32[1,16,2]{1,2,0:T(2,128)}, u32[]{:S(2)}) %copy-start) | copy-done | bytes 152
  9.0 0.1 copy.15
  9.1 0.1 fusion.2
  9.2 1.8 %bitcast_multiply_fusion = f32[1,16,2,16,128]{4,3,2,0,1:T(8,128)} fusion(f32[1,16,2,16,128]{4,3,2,1,0:T(8,128)} %param.4, f32[16,2,16]{2,1,0:T(2,128)S(1)} %fusion.2), kind=kLoop, calls=%fused_computation.1 | loop fusion | flops 65536 | bytes 526336 | tf_op jit(solution)/shard_map/mul | solution.py:14
  11.0 4.7 %all-to-all-done = s32[1,16,2,16]{3,2,0,1:T(2,128)S(1)} async-done(((s32[1,16,2,16]{3,2,0,1:T(2,128)}), s32[1,16,2,16]{3,2,0,1:T(2,128)S(1)}, u32[]{:S(2)}, u32[]{:S(2)}) %all-to-all-start) | async-done | bytes 2080 | tf_op jit(solution)/shard_map/all_to_all | solution.py:24
  15.7 0.1 reshape.45
  15.8 3.7 %all_to_all.42 = s32[2,1,256]{2,1,0:T(1,128)S(1)} all-to-all(s32[2,1,256]{2,1,0:T(1,128)S(1)} %reshape.45), channel_id=1, replica_groups=mesh['row'=16,'col'=2] {'col'}, dimensions={0} | all-to-all | bytes 4096 | tf_op jit(solution)/shard_map/all_to_all | solution.py:23
  19.5 0.0 copy-start.1
  19.5 3.7 %all-to-all-start.2 = ((f32[1,16,2,16,128]{4,3,2,0,1:T(8,128)}), f32[1,16,2,16,128]{4,3,2,0,1:T(8,128)S(1)}, u32[]{:S(2)}, u32[]{:S(2)}) async-start(f32[1,16,2,16,128]{4,3,2,0,1:T(8,128)} %bitcast_multiply_fusion), calls=%async_computation.2 | async-start | bytes 524288 | tf_op jit(solution)/shard_map/all_to_all | solution.py:17
  23.1 0.0 copy-done.1
  23.2 0.5 %broadcast.9 = s32[]{:T(128)} broadcast(s32[]{:T(128)} %constant.8), dimensions={} | broadcast | bytes 8 | tf_op jit(solution)/shard_map/all_to_all | solution.py:23
  23.7 0.7 %reduce = s32[2,256]{1,0:T(2,128)S(1)} reduce(s32[2,1,256]{2,1,0:T(1,128)S(1)} %all_to_all.42, s32[]{:T(128)} %broadcast.9), dimensions={1}, to_apply=%all_to_all.14.reduce_sub_computation | reduce | bytes 4100 | tf_op jit(solution)/shard_map/all_to_all | solution.py:23
  24.3 0.1 reshape.46
  24.4 0.1 reshape.36
  24.5 9.0 %all-to-all-done.2 = f32[1,16,2,16,128]{4,3,2,0,1:T(8,128)S(1)} async-done(((f32[1,16,2,16,128]{4,3,2,0,1:T(8,128)}), f32[1,16,2,16,128]{4,3,2,0,1:T(8,128)S(1)}, u32[]{:S(2)}, u32[]{:S(2)}) %all-to-all-start.2) | async-done | bytes 262176 | tf_op jit(solution)/shard_map/all_to_all | solution.py:17
  33.6 3.9 %all_to_all.43 = f32[16,1,2,16,128]{4,3,0,1,2:T(8,128)S(1)} all-to-all(f32[16,1,2,16,128]{4,3,0,1,2:T(8,128)S(1)} %copy.17), channel_id=1, replica_groups=mesh['row'=16,'col'=2] {'col'}, dimensions={2} | all-to-all | bytes 524288 | tf_op jit(solution)/shard_map/all_to_all | solution.py:16
  37.5 2.3 %scatter_custom_fusion = f32[256,128]{1,0:T(8,128)S(1)} fusion(s32[512]{0:T(512)S(1)} %reshape.36, f32[512,128]{1,0:T(8,128)S(1)} %bitcast.14, f32[]{:T(128)} %constant.0.clone.1), kind=kCustom, calls=%fused_computation.3 | custom fusion | flops 65536 | bytes 131076 | tf_op jit(solution)/shard_map/scatter-add | solution.py:31
  39.8 0.8 %broadcast_divide_fusion = f32[256,128]{1,0:T(8,128)} fusion(f32[256,128]{1,0:T(8,128)S(1)} %scatter_custom_fusion, f32[256]{0:T(256)S(1)} %maximum_convert_fusion), kind=kLoop, calls=%fused_computation.2 | loop fusion | flops 32768 | bytes 263168 | tf_op jit(solution)/shard_map/div | solution.py:35
  (5 shorter events, 0.1 us)
Async XLA Ops:
  0.0 15.7 %all-to-all-start = ((s32[1,16,2,16]{3,2,0,1:T(2,128)}), s32[1,16,2,16]{3,2,0,1:T(2,128)S(1)}, u32[]{:S(2)}, u32[]{:S(2)}) async-start(s32[1,16,2,16]{3,2,0,1:T(2,128)} %bitcast.18), calls=%async_computation | async-start | bytes 32768 | tf_op jit(solution)/shard_map/all_to_all | solution.py:24
  8.3 0.7 %copy-start = (s32[1,16,2]{1,2,0:T(2,128)S(1)}, s32[1,16,2]{1,2,0:T(2,128)}, u32[]{:S(2)}) copy-start(s32[1,16,2]{1,2,0:T(2,128)} %param.6) | copy-start | bytes 388
  19.5 3.7 %copy-start.1 = (s32[256]{0:T(256)S(1)}, s32[256]{0:T(256)}, u32[]{:S(2)}) copy-start(s32[256]{0:T(256)} %param.7) | copy-start | bytes 3076
  19.5 14.1 %all-to-all-start.2 = ((f32[1,16,2,16,128]{4,3,2,0,1:T(8,128)}), f32[1,16,2,16,128]{4,3,2,0,1:T(8,128)S(1)}, u32[]{:S(2)}, u32[]{:S(2)}) async-start(f32[1,16,2,16,128]{4,3,2,0,1:T(8,128)} %bitcast_multiply_fusion), calls=%async_computation.2 | async-start | bytes 524288 | tf_op jit(solution)/shard_map/all_to_all | solution.py:17
where the time goes:
time: 41 us; the launch traced here: 40.6 us
  waiting for transfers between devices  13.7 us (33%)
  starting transfers between devices  12 us (29%)
  blocking collectives  7.63 us (19%)
  other arithmetic  5.58 us (14%)
  local copies, waits for them, and re-layouts  1.57 us (4%)
    all_to_all x1, waiting for transfers between devices, body(): lax.all_to_all(masked, 'row', split_axis=1, concat_axis=0, tiled=True)  9.04 us
    all_to_all x1, starting transfers between devices, body(): lax.all_to_all(dst_local, 'row', split_axis=1, concat_axis=0, tiled=True)  8.34 us
    all_to_all x1, waiting for transfers between devices, body(): lax.all_to_all(dst_local, 'row', split_axis=1, concat_axis=0, tiled=True)  4.7 us
    all_to_all x1, blocking collectives, body(): lax.all_to_all(lax.all_to_all(masked, 'row', split_axis=1, concat_axis=0,...  3.94 us
    all_to_all x1, blocking collectives, body(): lax.all_to_all(lax.all_to_all(dst_local, 'row', split_axis=1, concat_axis...  3.69 us
    all_to_all x1, starting transfers between devices, body(): lax.all_to_all(masked, 'row', split_axis=1, concat_axis=0, tiled=True)  3.66 us
    scatter-add x1, other arithmetic, body(): jax.ops.segment_sum(received.reshape(-1, width), labels.reshape(-1), num_...  2.29 us
    mul x1, other arithmetic, body(): masked = messages * alive_mask[..., None]  1.78 us
  transfers between devices with their start and end apart: 2, of which 2 were waited for; matrix products, arithmetic and copies ran while one was open for 8% of the time, Pallas kernels for 0%

commit v1 on v0

v1 whole, which is shorter than its diff:
```python
import jax
import jax.numpy as jnp
from jax import lax
from jax.experimental import pallas as pl
from jax.experimental.pallas import tpu as pltpu
from jax.sharding import PartitionSpec as P

LANES = 128
SUBLANES = 8


def general(messages, dst_local, counts, degrees):
    slots = messages.shape[3]
    width = messages.shape[4]
    owned = degrees.shape[0]
    slot_index = lax.broadcasted_iota(jnp.int32, counts.shape + (slots,), 3)
    alive_mask = (slot_index < counts[..., None]).astype(jnp.float32)
    masked = messages * alive_mask[..., None]

    def exchange(x):
        x = lax.all_to_all(x, "row", split_axis=1, concat_axis=0, tiled=True)
        return lax.all_to_all(x, "col", split_axis=2, concat_axis=1, tiled=True)

    received, labels = exchange(masked), exchange(dst_local)
    summed = jax.ops.segment_sum(received.reshape(-1, width), labels.reshape(-1), num_segments=owned)
    scale = jnp.maximum(degrees, 1).astype(jnp.float32)
    return summed / scale[:, None]


def meeting_order(rows):
    first = rows * 5 // 8
    return [first] + [r for r in range(1, rows) if r != first] + [0]


def pack_kernel(order, owned, counts_ref, dst_ref, messages_ref, out_ref):
    groups, _, slots, width = messages_ref.shape
    half = slots // 2
    live = slots + half
    pitch = live + 1
    lane = lax.broadcasted_iota(jnp.int32, (groups, width), 1)
    group = lax.broadcasted_iota(jnp.int32, (groups, width), 0)
    full = [counts_ref[0, g] == slots for g in range(groups)]
    full_rows = jnp.zeros((groups, width), jnp.int32)
    for g in range(groups):
        full_rows = jnp.where(group == g, full[g].astype(jnp.int32), full_rows)
    fill = jnp.zeros((groups, width - slots), jnp.int32)
    first = jnp.concatenate([dst_ref[pl.ds(0, groups, stride=2), :], fill], axis=1)
    second = jnp.concatenate([dst_ref[pl.ds(1, groups, stride=2), :], fill], axis=1) + owned
    by_half = pltpu.roll(second, half, 1)
    by_full = pltpu.roll(second, slots, 1)
    when_full = jnp.where(lane < slots, first, by_full)
    when_half = jnp.where(lane < half, first, by_half)
    labels = jnp.where(full_rows == 1, when_full, when_half).astype(jnp.float32)
    for place, g in enumerate(order):
        base = place * pitch
        a0 = messages_ref[g, 0, :half, :]
        a1 = messages_ref[g, 0, half:, :]
        b0 = messages_ref[g, 1, :half, :]
        b1 = messages_ref[g, 1, half:, :]
        out_ref[base : base + half, :] = a0
        out_ref[base + half : base + slots, :] = jnp.where(full[g], a1, b0)
        out_ref[base + slots : base + live, :] = jnp.where(full[g], b0, b1)
        out_ref[base + live : base + pitch, :] = labels[g : g + 1, :]


def sum_kernel(rows, owned, received_ref, own_ref, other_ref):
    width = received_ref.shape[1]
    pitch = received_ref.shape[0] // rows
    live = pitch - 1
    total = rows * live
    labels = received_ref[pl.ds(live, rows, stride=pitch), :].astype(jnp.int32)
    left = live
    while left:
        step = min(left, (width - 1) // (rows - 1))
        labels = pltpu.roll(labels, 0, 1, stride=step, stride_axis=0)
        left -= step
    place = lax.broadcasted_iota(jnp.int32, (rows, width), 0)
    lane = lax.broadcasted_iota(jnp.int32, (rows, width), 1)
    slot = lax.rem(lane - lax.rem(place * live, width) + width, width)
    position = place * live + slot
    parts = []
    for block in range(total // width):
        inside = (slot < live) & (position >= block * width) & (position < (block + 1) * width)
        parts.append(jnp.sum(jnp.where(inside, labels, 0), axis=0, keepdims=True))
    label = jnp.concatenate(parts, axis=1)
    values = jnp.concatenate([received_ref[p * pitch : p * pitch + live, :] for p in range(rows)], axis=0)
    high = values.astype(jnp.bfloat16)
    low = (values - high.astype(jnp.float32)).astype(jnp.bfloat16)
    both = jnp.concatenate([high, low], axis=1)
    vertex = lax.broadcasted_iota(jnp.int32, (owned, total), 0)
    core = lax.axis_index("col")
    for ref, side in ((other_ref, 1 - core), (own_ref, core)):
        hot = (vertex == label - side * owned).astype(jnp.float32).astype(jnp.bfloat16)
        sums = jnp.dot(hot, both, preferred_element_type=jnp.float32)
        ref[...] = sums[:, :width] + sums[:, width:]


def paired(rows, messages, dst_local, counts, degrees):
    _, groups, subs, slots, width = messages.shape
    owned = degrees.shape[0]
    pitch = slots + slots // 2 + 1
    order = meeting_order(rows)
    vmem = pl.BlockSpec(memory_space=pltpu.VMEM)
    packed = pl.pallas_call(
        lambda *refs: pack_kernel(order, owned, *refs),
        out_shape=jax.ShapeDtypeStruct((groups * pitch, width), jnp.float32),
        in_specs=[pl.BlockSpec(memory_space=pltpu.SMEM), vmem, vmem],
        out_specs=vmem,
        name="pack",
    )(counts.reshape(groups, subs).T, dst_local.reshape(groups * subs, slots), messages[0])
    received = lax.all_to_all(
        packed.reshape(groups * pitch, 1, width),
        "row",
        split_axis=0,
        concat_axis=0,
        tiled=True,
        axis_index_groups=[order],
    ).reshape(groups * pitch, width)
    own, other = pl.pallas_call(
        lambda *refs: sum_kernel(rows, owned, *refs),
        out_shape=[jax.ShapeDtypeStruct((owned, width), jnp.float32)] * 2,
        in_specs=[vmem],
        out_specs=[vmem, vmem],
        name="sum_slots",
    )(received)
    mine = lax.ppermute(other, "col", [(0, 1), (1, 0)])
    scale = jnp.maximum(degrees, 1).astype(jnp.float32)
    return (own + mine) / scale[:, None]


def solution(mesh):
    rows, cols = mesh.shape["row"], mesh.shape["col"]

    def body(messages, dst_local, counts, degrees):
        subs, slots, width = messages.shape[2:]
        live = slots + slots // 2
        fits = width == LANES and slots % (2 * SUBLANES) == 0 and rows * live % width == 0
        if subs == cols == 2 and fits and rows <= 16:
            return paired(rows, messages, dst_local, counts, degrees)
        return general(messages, dst_local, counts, degrees)

    in_specs = (
        P(("row", "col"), None, None, None, None),
        P(("row", "col"), None, None, None),
        P(("row", "col"), None, None),
        P(("row", "col")),
    )
    out_specs = P(("row", "col"), None)
    return jax.shard_map(body, mesh=mesh, in_specs=in_specs, out_specs=out_specs, check_vma=False)
```

time: 41 us -> 22.1 us (0.54)
  waiting for transfers between devices: 13.7 us -> 0.88 us
  starting transfers between devices: 12 us -> 0.01 us
  blocking collectives: 7.63 us -> 14.7 us
  other arithmetic: 5.58 us -> 1.67 us
  Pallas kernels: 0 us -> 3.87 us
  local copies, waits for them, and re-layouts: 1.57 us -> 0.68 us
    all_to_all x2 -> x0, waiting for transfers between devices: 13.7 us -> none  [the longest x1 9.04 us: body(): lax.all_to_all(masked, 'row', split_axis=1, concat_axis=0, tiled=True)]
    all_to_all x2 -> x0, starting transfers between devices: 12 us -> none  [the longest x1 8.34 us: body(): lax.all_to_all(dst_local, 'row', split_axis=1, concat_axis=0, tiled=True)]
    all_to_all x2 -> x1, blocking collectives: 7.63 us -> 14.7 us  [paired(): lax.all_to_all(packed.reshape(groups * pitch, 1, width), 'row', split_axi...]
    pallas_call x0 -> x2, Pallas kernels: none -> 3.87 us  [the longest x1 2.14 us: paired(): pl.pallas_call(lambda *refs: sum_kernel(rows, owned, *refs), out_shape=[j...]
    scatter-add x1 -> x0, other arithmetic: 2.29 us -> none  [body(): jax.ops.segment_sum(received.reshape(-1, width), labels.reshape(-1), num_...]
    mul x1 -> x0, other arithmetic: 1.78 us -> none  [body(): masked = messages * alive_mask[..., None]]
    div x1, other arithmetic: 0.76 us -> 1.67 us  [paired(): return (own + mine) / scale[:, None]]
    ppermute x0 -> x1, waiting for transfers between devices: none -> 0.88 us  [paired(): mine = lax.ppermute(other, 'col', [(0, 1), (1, 0)])]
  transfers between devices with their start and end apart: 2 -> 1, of which waited for: 2 -> 1; matrix products, arithmetic and copies ran while one was open for 8% -> 0% of each run, Pallas kernels for 0% -> 0%
where the time goes in v1:
time: 22.1 us; the launch traced here: 21.8 us
  blocking collectives  14.7 us (67%)
  Pallas kernels  3.87 us (18%)
  other arithmetic  1.67 us (8%)
  waiting for transfers between devices  0.88 us (4%)
  local copies, waits for them, and re-layouts  0.68 us (3%)
    all_to_all x1, blocking collectives, paired(): lax.all_to_all(packed.reshape(groups * pitch, 1, width), 'row', split_axi...  14.7 us
    pallas_call x1, Pallas kernels, paired(): pl.pallas_call(lambda *refs: sum_kernel(rows, owned, *refs), out_shape=[j...  2.14 us
    pallas_call x1, Pallas kernels, paired(): pl.pallas_call(lambda *refs: pack_kernel(order, owned, *refs), out_shape=...  1.73 us
    div x1, other arithmetic, paired(): return (own + mine) / scale[:, None]  1.67 us
    ppermute x1, waiting for transfers between devices, paired(): mine = lax.ppermute(other, 'col', [(0, 1), (1, 0)])  0.88 us
    unnamed x2, local copies, waits for them, and re-layouts  0.68 us
  transfers between devices with their start and end apart: 1, of which 1 were waited for; matrix products, arithmetic and copies ran while one was open for 0% of the time, Pallas kernels for 0%

profile of v1, /device:TPU:0, one launch (start us, length us, event | category | flops | bytes accessed | tf_op | source)
XLA Modules:
  0.0 21.8 jit_solution(4202262254717003787)
XLA Ops:
  0.0 1.7 %pack.1 = f32[400,128]{1,0:T(8,128)} custom-call(s32[2,16]{1,0:T(2,128)} %bitcast.13, s32[32,16]{1,0:T(8,128)} %bitcast.12, f32[16,2,16,128]{3,2,1,0:T(8,128)} %bitcast.11), custom_call_target="tpu_custom_call" | custom-call | tf_op jit(solution)/shard_map/pack/pallas_call | solution.py:104
  1.7 14.7 %all_to_all.5 = f32[400,1,128]{2,1,0:T(1,128)} all-to-all(f32[400,1,128]{2,1,0:T(1,128)} %bitcast.10), channel_id=1, replica_groups={{20,2,4,6,8,10,12,14,16,18,22,24,26,28,30,0},{21,3,5,7,9,11,13,15,17,19..., dimensions={0} | all-to-all | bytes 409600 | tf_op jit(solution)/shard_map/all_to_all | solution.py:111
  16.4 2.1 %sum_slots.1 = (f32[256,128]{1,0:T(8,128)}, f32[256,128]{1,0:T(8,128)}) custom-call(f32[400,128]{1,0:T(8,128)} %bitcast.9), custom_call_target="tpu_custom_call" | custom-call | tf_op jit(solution)/shard_map/sum_slots/pallas_call | solution.py:119
  18.5 0.0 copy-start
  18.5 0.0 collective-permute-start
  18.5 0.7 %copy-done = s32[256]{0:T(256)S(1)} copy-done((s32[256]{0:T(256)S(1)}, s32[256]{0:T(256)}, u32[]{:S(2)}) %copy-start) | copy-done | bytes 1048
  19.2 0.9 %collective-permute-done = f32[256,128]{1,0:T(8,128)S(1)} collective-permute-done((f32[256,128]{1,0:T(8,128)}, f32[256,128]{1,0:T(8,128)S(1)}, u32[]{:S(2)}, u32[]{:S(2)}) %collective-permute-start) | collective-permute-done | bytes 131104 | tf_op jit(solution)/shard_map/ppermute | solution.py:126
  20.1 1.7 %add_divide_fusion = f32[256,128]{1,0:T(8,128)} fusion(f32[256,128]{1,0:T(8,128)} %get-tuple-element.7, f32[256,128]{1,0:T(8,128)S(1)} %collective-permute-done, f32[256]{0:T(256)S(1)} %maximum_convert_fusion), kind=kLoop, calls=%fused_computation | loop fusion | flops 65536 | bytes 394240 | tf_op jit(solution)/shard_map/div | solution.py:128
  (1 shorter events, 0.0 us)
Async XLA Ops:
  18.5 0.7 %copy-start = (s32[256]{0:T(256)S(1)}, s32[256]{0:T(256)}, u32[]{:S(2)}) copy-start(s32[256]{0:T(256)} %param.7) | copy-start | bytes 3076
  18.5 1.6 %collective-permute-start = (f32[256,128]{1,0:T(8,128)}, f32[256,128]{1,0:T(8,128)S(1)}, u32[]{:S(2)}, u32[]{:S(2)}) collective-permute-start(f32[256,128]{1,0:T(8,128)} %get-tuple-element.8), channel_id=1, source_target_pairs={{0,1},{1,0},{2,3},{3,2},{4,5},{5,4},{6,7},{7,6},{8,9},{9,8},{10,11... | collective-permute-start | bytes 393224 | tf_op jit(solution)/shard_map/ppermute | solution.py:126

commit v2 on v1

--- a/solution.py
+++ b/solution.py
@@ -7,6 +7,7 @@
 
 LANES = 128
 SUBLANES = 8
+SMALL = pltpu.CompilerParams(vmem_limit_bytes=8 << 20)
 
 
 def general(messages, dst_local, counts, degrees):
@@ -27,16 +28,30 @@
     return summed / scale[:, None]
 
 
+def in_hbm(x):
+    return pltpu.with_memory_space_constraint(x, pltpu.HBM)
+
+
 def meeting_order(rows):
     first = rows * 5 // 8
     return [first] + [r for r in range(1, rows) if r != first] + [0]
 
 
-def pack_kernel(order, owned, counts_ref, dst_ref, messages_ref, out_ref):
+def pack_kernel(order, owned, counts_hbm, dst_hbm, messages_hbm, out_ref, counts_ref, dst_ref, messages_ref, sems):
+    fetches = [
+        pltpu.make_async_copy(source, target, sems.at[i])
+        for i, (source, target) in enumerate(
+            ((counts_hbm, counts_ref), (dst_hbm, dst_ref), (messages_hbm, messages_ref))
+        )
+    ]
+    for fetch in fetches:
+        fetch.start()
     groups, _, slots, width = messages_ref.shape
     half = slots // 2
     live = slots + half
     pitch = live + 1
+    for fetch in fetches[:2]:
+        fetch.wait()
     lane = lax.broadcasted_iota(jnp.int32, (groups, width), 1)
     group = lax.broadcasted_iota(jnp.int32, (groups, width), 0)
     full = [counts_ref[0, g] == slots for g in range(groups)]
@@ -51,6 +66,7 @@
     when_full = jnp.where(lane < slots, first, by_full)
     when_half = jnp.where(lane < half, first, by_half)
     labels = jnp.where(full_rows == 1, when_full, when_half).astype(jnp.float32)
+    fetches[2].wait()
     for place, g in enumerate(order):
         base = place * pitch
         a0 = messages_ref[g, 0, :half, :]
@@ -63,7 +79,7 @@
         out_ref[base + live : base + pitch, :] = labels[g : g + 1, :]
 
 
-def sum_kernel(rows, owned, received_ref, own_ref, other_ref):
+def slot_values(rows, received_ref, both_ref, label_ref):
     width = received_ref.shape[1]
     pitch = received_ref.shape[0] // rows
     live = pitch - 1
@@ -87,12 +103,44 @@
     high = values.astype(jnp.bfloat16)
     low = (values - high.astype(jnp.float32)).astype(jnp.bfloat16)
     both = jnp.concatenate([high, low], axis=1)
-    vertex = lax.broadcasted_iota(jnp.int32, (owned, total), 0)
-    core = lax.axis_index("col")
-    for ref, side in ((other_ref, 1 - core), (own_ref, core)):
-        hot = (vertex == label - side * owned).astype(jnp.float32).astype(jnp.bfloat16)
-        sums = jnp.dot(hot, both, preferred_element_type=jnp.float32)
-        ref[...] = sums[:, :width] + sums[:, width:]
+    both_ref[...] = both
+    label_ref[...] = jnp.broadcast_to(label, label_ref.shape)
+    return both, label
+
+
+def range_sums(owned, side, both, label):
+    width = both.shape[1] // 2
+    vertex = lax.broadcasted_iota(jnp.int32, (owned, both.shape[0]), 0)
+    hot = (vertex == label - side * owned).astype(jnp.float32).astype(jnp.bfloat16)
+    sums = jnp.dot(hot, both, preferred_element_type=jnp.float32)
+    return sums[:, :width] + sums[:, width:]
+
+
+def other_kernel(rows, owned, received_ref, other_ref, both_ref, label_ref):
+    both, label = slot_values(rows, received_ref, both_ref, label_ref)
+    other_ref[...] = range_sums(owned, 1 - lax.axis_index("col"), both, label)
+
+
+def own_kernel(owned, both_ref, label_ref, degrees_ref, own_ref, share_ref):
+    width = own_ref.shape[1]
+    sums = range_sums(owned, lax.axis_index("col"), both_ref[...], label_ref[0:1, :])
+    for start in range(0, owned, width):
+        scale = jnp.maximum(degrees_ref[0:1, start : start + width], 1).astype(jnp.float32)
+        share = jnp.transpose(jnp.broadcast_to(1.0 / scale, (width, width)))
+        share_ref[start : start + width, :] = share
+        own_ref[start : start + width, :] = sums[start : start + width, :] * share
+
+
+def last_kernel(pieces, own_ref, mine_ref, share_ref, out_hbm, out_ref, sems):
+    size = out_ref.shape[0] // pieces
+    copies = []
+    for i in range(pieces):
+        piece = slice(i * size, (i + 1) * size)
+        out_ref[piece, :] = own_ref[piece, :] + mine_ref[piece, :] * share_ref[piece, :]
+        copies.append(pltpu.make_async_copy(out_ref.at[piece, :], out_hbm.at[piece, :], sems.at[i]))
+        copies[-1].start()
+    for copy in copies:
+        copy.wait()
 
 
 def paired(rows, messages, dst_local, counts, degrees):
@@ -100,14 +148,23 @@
     owned = degrees.shape[0]
     pitch = slots + slots // 2 + 1
     order = meeting_order(rows)
+    total = rows * (pitch - 1)
     vmem = pl.BlockSpec(memory_space=pltpu.VMEM)
+    hbm = pl.BlockSpec(memory_space=pltpu.HBM)
     packed = pl.pallas_call(
         lambda *refs: pack_kernel(order, owned, *refs),
         out_shape=jax.ShapeDtypeStruct((groups * pitch, width), jnp.float32),
-        in_specs=[pl.BlockSpec(memory_space=pltpu.SMEM), vmem, vmem],
+        in_specs=[hbm, hbm, hbm],
         out_specs=vmem,
+        scratch_shapes=[
+            pltpu.SMEM((subs, groups), jnp.int32),
+            pltpu.VMEM((groups * subs, slots), jnp.int32),
+            pltpu.VMEM((groups, subs, slots, width), jnp.float32),
+            pltpu.SemaphoreType.DMA((3,)),
+        ],
+        compiler_params=SMALL,
         name="pack",
-    )(counts.reshape(groups, subs).T, dst_local.reshape(groups * subs, slots), messages[0])
+    )(in_hbm(counts.reshape(groups, subs).T), in_hbm(dst_local.reshape(groups * subs, slots)), in_hbm(messages[0]))
     received = lax.all_to_all(
         packed.reshape(groups * pitch, 1, width),
         "row",
@@ -116,16 +173,39 @@
         tiled=True,
         axis_index_groups=[order],
     ).reshape(groups * pitch, width)
-    own, other = pl.pallas_call(
-        lambda *refs: sum_kernel(rows, owned, *refs),
-        out_shape=[jax.ShapeDtypeStruct((owned, width), jnp.float32)] * 2,
+    partial = jax.ShapeDtypeStruct((owned, width), jnp.float32)
+    other, both, label = pl.pallas_call(
+        lambda *refs: other_kernel(rows, owned, *refs),
+        out_shape=[
+            partial,
+            jax.ShapeDtypeStruct((total, 2 * width), jnp.bfloat16),
+            jax.ShapeDtypeStruct((SUBLANES, total), jnp.int32),
+        ],
         in_specs=[vmem],
-        out_specs=[vmem, vmem],
-        name="sum_slots",
+        out_specs=[vmem] * 3,
+        compiler_params=SMALL,
+        name="other_sums",
     )(received)
     mine = lax.ppermute(other, "col", [(0, 1), (1, 0)])
-    scale = jnp.maximum(degrees, 1).astype(jnp.float32)
-    return (own + mine) / scale[:, None]
+    own, share = pl.pallas_call(
+        lambda *refs: own_kernel(owned, *refs),
+        out_shape=[partial, partial],
+        in_specs=[vmem] * 3,
+        out_specs=[vmem] * 2,
+        compiler_params=SMALL,
+        cost_estimate=pl.CostEstimate(flops=4 * owned * total * width, bytes_accessed=1 << 20, transcendentals=0),
+        name="own_sums",
+    )(both, label, degrees.reshape(1, owned))
+    pieces = 4
+    return pl.pallas_call(
+        lambda *refs: last_kernel(pieces, *refs),
+        out_shape=partial,
+        in_specs=[vmem] * 3,
+        out_specs=hbm,
+        scratch_shapes=[pltpu.VMEM((owned, width), jnp.float32), pltpu.SemaphoreType.DMA((pieces,))],
+        compiler_params=SMALL,
+        name="mean",
+    )(own, mine, share)
 
 
 def solution(mesh):

time: 22.1 us -> 17.6 us (0.80)
  other arithmetic: 1.67 us -> 0 us
  Pallas kernels: 3.87 us -> 2.33 us
  blocking collectives: 14.7 us -> 13.9 us
  waiting for transfers between devices: 0.88 us -> 0.42 us
    div x1 -> x0, other arithmetic: 1.67 us -> none  [paired(): return (own + mine) / scale[:, None]]
    pallas_call x1 -> x3, Pallas kernels: 2.14 us -> 1.32 us  [the longest x1 0.69 us: paired(): pl.pallas_call(lambda *refs: last_kernel(pieces, *refs), out_shape=partia...]
    all_to_all x1, blocking collectives: 14.7 us -> 13.9 us  [paired(): lax.all_to_all(packed.reshape(groups * pitch, 1, width), 'row', split_axi...]
    pallas_call x1, Pallas kernels: 1.73 us -> 1.01 us  [paired(): pl.pallas_call(lambda *refs: pack_kernel(order, owned, *refs), out_shape=...]
    ppermute x1, waiting for transfers between devices: 0.88 us -> 0.42 us  [paired(): mine = lax.ppermute(other, 'col', [(0, 1), (1, 0)])]
  transfers between devices with their start and end apart: 1 -> 1, of which waited for: 1 -> 1; matrix products, arithmetic and copies ran while one was open for 0% -> 0% of each run, Pallas kernels for 0% -> 1%
where the time goes in v2:
time: 17.6 us; the launch traced here: 17.4 us
  blocking collectives  13.9 us (79%)
  Pallas kernels  2.33 us (13%)
  local copies, waits for them, and re-layouts  0.67 us (4%)
  waiting for transfers between devices  0.42 us (2%)
    all_to_all x1, blocking collectives, paired(): lax.all_to_all(packed.reshape(groups * pitch, 1, width), 'row', split_axi...  13.9 us
    pallas_call x1, Pallas kernels, paired(): pl.pallas_call(lambda *refs: pack_kernel(order, owned, *refs), out_shape=...  1.01 us
    pallas_call x1, Pallas kernels, paired(): pl.pallas_call(lambda *refs: last_kernel(pieces, *refs), out_shape=partia...  0.69 us
    unnamed x2, local copies, waits for them, and re-layouts  0.67 us
    ppermute x1, waiting for transfers between devices, paired(): mine = lax.ppermute(other, 'col', [(0, 1), (1, 0)])  0.42 us
    pallas_call x1, Pallas kernels, paired(): pl.pallas_call(lambda *refs: other_kernel(rows, owned, *refs), out_shape=...  0.41 us
  transfers between devices with their start and end apart: 1, of which 1 were waited for; matrix products, arithmetic and copies ran while one was open for 0% of the time, Pallas kernels for 1%

profile of v2, /device:TPU:0, one launch (start us, length us, event | category | flops | bytes accessed | tf_op | source)
XLA Modules:
  0.0 17.4 jit_solution(14528108292091775842)
XLA Ops:
  0.0 1.0 %pack.1 = f32[400,128]{1,0:T(8,128)S(1)} custom-call(s32[2,16]{1,0:T(2,128)} %bitcast.15, s32[32,16]{1,0:T(8,128)} %bitcast.14, f32[16,2,16,128]{3,2,1,0:T(8,128)} %bitcast.13), custom_call_target="tpu_custom_call" | custom-call | tf_op jit(solution)/shard_map/pack/pallas_call | solution.py:154
  1.0 13.9 %all_to_all.5 = f32[400,1,128]{2,1,0:T(1,128)S(1)} all-to-all(f32[400,1,128]{2,1,0:T(1,128)S(1)} %bitcast.11), channel_id=1, replica_groups={{20,2,4,6,8,10,12,14,16,18,22,24,26,28,30,0},{21,3,5,7,9,11,13,15,17,19..., dimensions={0} | all-to-all | bytes 409600 | tf_op jit(solution)/shard_map/all_to_all | solution.py:168
  14.9 0.4 %other_sums.1 = (f32[256,128]{1,0:T(8,128)S(1)}, bf16[384,256]{1,0:T(8,128)(2,1)S(1)}, s32[8,384]{1,0:T(8,128)S(1)}) custom-call(f32[400,128]{1,0:T(8,128)S(1)} %bitcast.10), custom_call_target="tpu_custom_call" | custom-call | tf_op jit(solution)/shard_map/other_sums/pallas_call | solution.py:177
  15.3 0.1 collective-permute-start
  15.4 0.0 copy-start
  15.4 0.7 %copy-done = s32[256]{0:T(256)S(1)} copy-done((s32[256]{0:T(256)S(1)}, s32[256]{0:T(256)}, u32[]{:S(2)}) %copy-start) | copy-done | bytes 1048
  16.1 0.2 %own_sums.1 = (f32[256,128]{1,0:T(8,128)S(1)}, f32[256,128]{1,0:T(8,128)S(1)}) custom-call(bf16[384,256]{1,0:T(8,128)(2,1)S(1)} %get-tuple-element.10.refs_0_, s32[8,384]{1,0:T(8,128)S(1)} %get-tuple-element.11.refs_1_, s32[1,256]{1,0:T(1,128)S(1)} %bitcast.12), custom_call_target="tpu_custom_call" | custom-call | flops 50331648 | bytes 1048576 | tf_op jit(solution)/shard_map/own_sums/pallas_call | solution.py:190
  16.3 0.4 %collective-permute-done.refs_1_ = f32[256,128]{1,0:T(8,128)S(1)} collective-permute-done((f32[256,128]{1,0:T(8,128)S(1)}, f32[256,128]{1,0:T(8,128)S(1)}, u32[]{:S(2)}, u32[]{:S(2)}) %collective-permute-start) | collective-permute-done | bytes 131104 | tf_op jit(solution)/shard_map/ppermute | solution.py:189
  16.8 0.7 %mean.1 = f32[256,128]{1,0:T(8,128)} custom-call(f32[256,128]{1,0:T(8,128)S(1)} %get-tuple-element.12.refs_0_, f32[256,128]{1,0:T(8,128)S(1)} %collective-permute-done.refs_1_, f32[256,128]{1,0:T(8,128)S(1)} %get-tuple-element.14.refs_2_), custom_call_target="tpu_custom_call" | custom-call | tf_op jit(solution)/shard_map/mean/pallas_call | solution.py:200
Async XLA Ops:
  15.3 1.4 %collective-permute-start = (f32[256,128]{1,0:T(8,128)S(1)}, f32[256,128]{1,0:T(8,128)S(1)}, u32[]{:S(2)}, u32[]{:S(2)}) collective-permute-start(f32[256,128]{1,0:T(8,128)S(1)} %get-tuple-element.13), channel_id=1, source_target_pairs={{0,1},{1,0},{2,3},{3,2},{4,5},{5,4},{6,7},{7,6},{8,9},{9,8},{10,11... | collective-permute-start | bytes 393224 | tf_op jit(solution)/shard_map/ppermute | solution.py:189
  15.4 0.7 %copy-start = (s32[256]{0:T(256)S(1)}, s32[256]{0:T(256)}, u32[]{:S(2)}) copy-start(s32[256]{0:T(256)} %param.7) | copy-start | bytes 3076

commit v3 on v2

--- a/solution.py
+++ b/solution.py
@@ -32,9 +32,17 @@
     return pltpu.with_memory_space_constraint(x, pltpu.HBM)
 
 
+ORDERS = {16: (11, 8, 5, 3, 13, 14, 4, 2, 15, 12, 7, 9, 10, 1, 6, 0)}
+
+
 def meeting_order(rows):
-    first = rows * 5 // 8
-    return [first] + [r for r in range(1, rows) if r != first] + [0]
+    first = rows * 3 // 4 - 1
+    return ORDERS.get(rows, (first, *(r for r in range(1, rows) if r != first), 0))
+
+
+def exchange_groups(order, cols):
+    swap = [int(2 * r >= len(order)) for r in order]
+    return [[r * cols + (c ^ s) for r, s in zip(order, swap)] for c in range(cols)]
 
 
 def pack_kernel(order, owned, counts_hbm, dst_hbm, messages_hbm, out_ref, counts_ref, dst_ref, messages_ref, sems):
@@ -167,11 +175,11 @@
     )(in_hbm(counts.reshape(groups, subs).T), in_hbm(dst_local.reshape(groups * subs, slots)), in_hbm(messages[0]))
     received = lax.all_to_all(
         packed.reshape(groups * pitch, 1, width),
-        "row",
+        ("row", "col"),
         split_axis=0,
         concat_axis=0,
         tiled=True,
-        axis_index_groups=[order],
+        axis_index_groups=exchange_groups(order, 2),
     ).reshape(groups * pitch, width)
     partial = jax.ShapeDtypeStruct((owned, width), jnp.float32)
     other, both, label = pl.pallas_call(

time: 17.6 us -> 16.5 us (0.937)
  blocking collectives: 13.9 us -> 12.4 us
  starting transfers between devices: 0.07 us -> 0.86 us
  waiting for transfers between devices: 0.42 us -> 0.08 us
    all_to_all x1, blocking collectives: 13.9 us -> 12.4 us  [paired(): lax.all_to_all(packed.reshape(groups * pitch, 1, width), ('row', 'col'),...]
    ppermute x1, starting transfers between devices: 0.07 us -> 0.86 us  [paired(): mine = lax.ppermute(other, 'col', [(0, 1), (1, 0)])]
    ppermute x1, waiting for transfers between devices: 0.42 us -> 0.08 us  [paired(): mine = lax.ppermute(other, 'col', [(0, 1), (1, 0)])]
where the time goes in v3:
time: 16.5 us; the launch traced here: 16.3 us
  blocking collectives  12.4 us (75%)
  Pallas kernels  2.33 us (14%)
  starting transfers between devices  0.86 us (5%)
  local copies, waits for them, and re-layouts  0.68 us (4%)
    all_to_all x1, blocking collectives, paired(): lax.all_to_all(packed.reshape(groups * pitch, 1, width), ('row', 'col'),...  12.4 us
    pallas_call x1, Pallas kernels, paired(): pl.pallas_call(lambda *refs: pack_kernel(order, owned, *refs), out_shape=...  1.01 us
    ppermute x1, starting transfers between devices, paired(): mine = lax.ppermute(other, 'col', [(0, 1), (1, 0)])  0.86 us
    pallas_call x1, Pallas kernels, paired(): pl.pallas_call(lambda *refs: last_kernel(pieces, *refs), out_shape=partia...  0.69 us
    unnamed x2, local copies, waits for them, and re-layouts  0.68 us
    pallas_call x1, Pallas kernels, paired(): pl.pallas_call(lambda *refs: other_kernel(rows, owned, *refs), out_shape=...  0.41 us
  transfers between devices with their start and end apart: 1, of which 1 were waited for; matrix products, arithmetic and copies ran while one was open for 0% of the time, Pallas kernels for 1%

profile of v3, /device:TPU:0, one launch (start us, length us, event | category | flops | bytes accessed | tf_op | source)
XLA Modules:
  0.0 16.3 jit_solution(9939752987054510466)
XLA Ops:
  0.0 1.0 %pack.1 = f32[400,128]{1,0:T(8,128)S(1)} custom-call(s32[2,16]{1,0:T(2,128)} %bitcast.15, s32[32,16]{1,0:T(8,128)} %bitcast.14, f32[16,2,16,128]{3,2,1,0:T(8,128)} %bitcast.13), custom_call_target="tpu_custom_call" | custom-call | tf_op jit(solution)/shard_map/pack/pallas_call | solution.py:162
  1.0 12.4 %all_to_all.5 = f32[400,1,128]{2,1,0:T(1,128)S(1)} all-to-all(f32[400,1,128]{2,1,0:T(1,128)S(1)} %bitcast.11), channel_id=1, replica_groups={{23,17,10,6,27,29,8,4,31,25,14,19,21,2,12,0},{22,16,11,7,26,28,9,5,30,2..., dimensions={0} | all-to-all | bytes 409600 | tf_op jit(solution)/shard_map/all_to_all | solution.py:176
  13.4 0.4 %other_sums.1 = (f32[256,128]{1,0:T(8,128)S(1)}, bf16[384,256]{1,0:T(8,128)(2,1)S(1)}, s32[8,384]{1,0:T(8,128)S(1)}) custom-call(f32[400,128]{1,0:T(8,128)S(1)} %bitcast.10), custom_call_target="tpu_custom_call" | custom-call | tf_op jit(solution)/shard_map/other_sums/pallas_call | solution.py:185
  13.8 0.9 %collective-permute-start = (f32[256,128]{1,0:T(8,128)S(1)}, f32[256,128]{1,0:T(8,128)S(1)}, u32[]{:S(2)}, u32[]{:S(2)}) collective-permute-start(f32[256,128]{1,0:T(8,128)S(1)} %get-tuple-element.13), channel_id=1, source_target_pairs={{0,1},{1,0},{2,3},{3,2},{4,5},{5,4},{6,7},{7,6},{8,9},{9,8},{10,11... | collective-permute-start | bytes 393224 | tf_op jit(solution)/shard_map/ppermute | solution.py:197
  14.7 0.0 copy-start
  14.7 0.7 %copy-done = s32[256]{0:T(256)S(1)} copy-done((s32[256]{0:T(256)S(1)}, s32[256]{0:T(256)}, u32[]{:S(2)}) %copy-start) | copy-done | bytes 1048
  15.3 0.2 %own_sums.1 = (f32[256,128]{1,0:T(8,128)S(1)}, f32[256,128]{1,0:T(8,128)S(1)}) custom-call(bf16[384,256]{1,0:T(8,128)(2,1)S(1)} %get-tuple-element.10.refs_0_, s32[8,384]{1,0:T(8,128)S(1)} %get-tuple-element.11.refs_1_, s32[1,256]{1,0:T(1,128)S(1)} %bitcast.12), custom_call_target="tpu_custom_call" | custom-call | flops 50331648 | bytes 1048576 | tf_op jit(solution)/shard_map/own_sums/pallas_call | solution.py:198
  15.6 0.1 collective-permute-done.refs_1_
  15.6 0.7 %mean.1 = f32[256,128]{1,0:T(8,128)} custom-call(f32[256,128]{1,0:T(8,128)S(1)} %get-tuple-element.12.refs_0_, f32[256,128]{1,0:T(8,128)S(1)} %collective-permute-done.refs_1_, f32[256,128]{1,0:T(8,128)S(1)} %get-tuple-element.14.refs_2_), custom_call_target="tpu_custom_call" | custom-call | tf_op jit(solution)/shard_map/mean/pallas_call | solution.py:208
Async XLA Ops:
  13.8 1.8 %collective-permute-start = (f32[256,128]{1,0:T(8,128)S(1)}, f32[256,128]{1,0:T(8,128)S(1)}, u32[]{:S(2)}, u32[]{:S(2)}) collective-permute-start(f32[256,128]{1,0:T(8,128)S(1)} %get-tuple-element.13), channel_id=1, source_target_pairs={{0,1},{1,0},{2,3},{3,2},{4,5},{5,4},{6,7},{7,6},{8,9},{9,8},{10,11... | collective-permute-start | bytes 393224 | tf_op jit(solution)/shard_map/ppermute | solution.py:197
  14.7 0.7 %copy-start = (s32[256]{0:T(256)S(1)}, s32[256]{0:T(256)}, u32[]{:S(2)}) copy-start(s32[256]{0:T(256)} %param.7) | copy-start | bytes 3076

commit v4 on v3

--- a/solution.py
+++ b/solution.py
@@ -7,6 +7,7 @@
 
 LANES = 128
 SUBLANES = 8
+FETCHES = 4
 SMALL = pltpu.CompilerParams(vmem_limit_bytes=8 << 20)
 
 
@@ -45,38 +46,52 @@
     return [[r * cols + (c ^ s) for r, s in zip(order, swap)] for c in range(cols)]
 
 
-def pack_kernel(order, owned, counts_hbm, dst_hbm, messages_hbm, out_ref, counts_ref, dst_ref, messages_ref, sems):
-    fetches = [
-        pltpu.make_async_copy(source, target, sems.at[i])
-        for i, (source, target) in enumerate(
-            ((counts_hbm, counts_ref), (dst_hbm, dst_ref), (messages_hbm, messages_ref))
-        )
-    ]
+def pack_kernel(order, *refs):
+    counts_hbm, dst_hbm, degrees_hbm, messages_hbm, out_ref, share_ref = refs[:6]
+    counts_ref, dst_ref, degrees_ref, messages_ref, sems = refs[6:]
+    groups, _, slots, width = messages_ref.shape
+    owned = degrees_ref.shape[1]
+    small = 3
+    pieces = sems.shape[0] - small
+    size = groups // pieces
+    sides = [(counts_hbm, counts_ref), (dst_hbm, dst_ref), (degrees_hbm, degrees_ref)]
+    for i in range(pieces):
+        piece = pl.ds(i * size, size)
+        sides.append((messages_hbm.at[piece], messages_ref.at[piece]))
+    fetches = [pltpu.make_async_copy(*side, sems.at[i]) for i, side in enumerate(sides)]
     for fetch in fetches:
         fetch.start()
-    groups, _, slots, width = messages_ref.shape
     half = slots // 2
     live = slots + half
     pitch = live + 1
-    for fetch in fetches[:2]:
-        fetch.wait()
+    row = lax.axis_index("row")
+    place = sum(jnp.where(row == r, p, 0) for p, r in enumerate(order))
     lane = lax.broadcasted_iota(jnp.int32, (groups, width), 1)
     group = lax.broadcasted_iota(jnp.int32, (groups, width), 0)
+    fill = jnp.zeros((groups, width - slots), jnp.int32)
+    for fetch in fetches[:small]:
+        fetch.wait()
     full = [counts_ref[0, g] == slots for g in range(groups)]
     full_rows = jnp.zeros((groups, width), jnp.int32)
     for g in range(groups):
         full_rows = jnp.where(group == g, full[g].astype(jnp.int32), full_rows)
-    fill = jnp.zeros((groups, width - slots), jnp.int32)
     first = jnp.concatenate([dst_ref[pl.ds(0, groups, stride=2), :], fill], axis=1)
     second = jnp.concatenate([dst_ref[pl.ds(1, groups, stride=2), :], fill], axis=1) + owned
     by_half = pltpu.roll(second, half, 1)
     by_full = pltpu.roll(second, slots, 1)
     when_full = jnp.where(lane < slots, first, by_full)
     when_half = jnp.where(lane < half, first, by_half)
-    labels = jnp.where(full_rows == 1, when_full, when_half).astype(jnp.float32)
-    fetches[2].wait()
-    for place, g in enumerate(order):
-        base = place * pitch
+    labels = jnp.where(lane < live, jnp.where(full_rows == 1, when_full, when_half), 0)
+    labels = pltpu.roll(labels.astype(jnp.float32), lax.rem(place * live, width), 1)
+    for p, g in enumerate(order):
+        out_ref[p * pitch + live : (p + 1) * pitch, :] = labels[g : g + 1, :]
+    for start in range(0, owned, width):
+        scale = jnp.maximum(degrees_ref[0:1, start : start + width], 1).astype(jnp.float32)
+        share_ref[start : start + width, :] = jnp.transpose(jnp.broadcast_to(1.0 / scale, (width, width)))
+    for g in range(groups):
+        if g % size == 0:
+            fetches[small + g // size].wait()
+        base = order.index(g) * pitch
         a0 = messages_ref[g, 0, :half, :]
         a1 = messages_ref[g, 0, half:, :]
         b0 = messages_ref[g, 1, :half, :]
@@ -84,7 +99,6 @@
         out_ref[base : base + half, :] = a0
         out_ref[base + half : base + slots, :] = jnp.where(full[g], a1, b0)
         out_ref[base + slots : base + live, :] = jnp.where(full[g], b0, b1)
-        out_ref[base + live : base + pitch, :] = labels[g : g + 1, :]
 
 
 def slot_values(rows, received_ref, both_ref, label_ref):
@@ -93,11 +107,6 @@
     live = pitch - 1
     total = rows * live
     labels = received_ref[pl.ds(live, rows, stride=pitch), :].astype(jnp.int32)
-    left = live
-    while left:
-        step = min(left, (width - 1) // (rows - 1))
-        labels = pltpu.roll(labels, 0, 1, stride=step, stride_axis=0)
-        left -= step
     place = lax.broadcasted_iota(jnp.int32, (rows, width), 0)
     lane = lax.broadcasted_iota(jnp.int32, (rows, width), 1)
     slot = lax.rem(lane - lax.rem(place * live, width) + width, width)
@@ -129,14 +138,9 @@
     other_ref[...] = range_sums(owned, 1 - lax.axis_index("col"), both, label)
 
 
-def own_kernel(owned, both_ref, label_ref, degrees_ref, own_ref, share_ref):
-    width = own_ref.shape[1]
+def own_kernel(owned, both_ref, label_ref, share_ref, own_ref):
     sums = range_sums(owned, lax.axis_index("col"), both_ref[...], label_ref[0:1, :])
-    for start in range(0, owned, width):
-        scale = jnp.maximum(degrees_ref[0:1, start : start + width], 1).astype(jnp.float32)
-        share = jnp.transpose(jnp.broadcast_to(1.0 / scale, (width, width)))
-        share_ref[start : start + width, :] = share
-        own_ref[start : start + width, :] = sums[start : start + width, :] * share
+    own_ref[...] = sums * share_ref[...]
 
 
 def last_kernel(pieces, own_ref, mine_ref, share_ref, out_hbm, out_ref, sems):
@@ -159,20 +163,27 @@
     total = rows * (pitch - 1)
     vmem = pl.BlockSpec(memory_space=pltpu.VMEM)
     hbm = pl.BlockSpec(memory_space=pltpu.HBM)
-    packed = pl.pallas_call(
-        lambda *refs: pack_kernel(order, owned, *refs),
-        out_shape=jax.ShapeDtypeStruct((groups * pitch, width), jnp.float32),
-        in_specs=[hbm, hbm, hbm],
-        out_specs=vmem,
+    partial = jax.ShapeDtypeStruct((owned, width), jnp.float32)
+    packed, share = pl.pallas_call(
+        lambda *refs: pack_kernel(order, *refs),
+        out_shape=[jax.ShapeDtypeStruct((groups * pitch, width), jnp.float32), partial],
+        in_specs=[hbm] * 4,
+        out_specs=[vmem] * 2,
         scratch_shapes=[
             pltpu.SMEM((subs, groups), jnp.int32),
             pltpu.VMEM((groups * subs, slots), jnp.int32),
+            pltpu.VMEM((1, owned), jnp.int32),
             pltpu.VMEM((groups, subs, slots, width), jnp.float32),
-            pltpu.SemaphoreType.DMA((3,)),
+            pltpu.SemaphoreType.DMA((3 + FETCHES,)),
         ],
         compiler_params=SMALL,
         name="pack",
-    )(in_hbm(counts.reshape(groups, subs).T), in_hbm(dst_local.reshape(groups * subs, slots)), in_hbm(messages[0]))
+    )(
+        in_hbm(counts.reshape(groups, subs).T),
+        in_hbm(dst_local.reshape(groups * subs, slots)),
+        in_hbm(degrees.reshape(1, owned)),
+        in_hbm(messages[0]),
+    )
     received = lax.all_to_all(
         packed.reshape(groups * pitch, 1, width),
         ("row", "col"),
@@ -181,7 +192,6 @@
         tiled=True,
         axis_index_groups=exchange_groups(order, 2),
     ).reshape(groups * pitch, width)
-    partial = jax.ShapeDtypeStruct((owned, width), jnp.float32)
     other, both, label = pl.pallas_call(
         lambda *refs: other_kernel(rows, owned, *refs),
         out_shape=[
@@ -195,15 +205,15 @@
         name="other_sums",
     )(received)
     mine = lax.ppermute(other, "col", [(0, 1), (1, 0)])
-    own, share = pl.pallas_call(
+    own = pl.pallas_call(
         lambda *refs: own_kernel(owned, *refs),
-        out_shape=[partial, partial],
+        out_shape=partial,
         in_specs=[vmem] * 3,
-        out_specs=[vmem] * 2,
+        out_specs=vmem,
         compiler_params=SMALL,
         cost_estimate=pl.CostEstimate(flops=4 * owned * total * width, bytes_accessed=1 << 20, transcendentals=0),
         name="own_sums",
-    )(both, label, degrees.reshape(1, owned))
+    )(both, label, share)
     pieces = 4
     return pl.pallas_call(
         lambda *refs: last_kernel(pieces, *refs),

time: 16.5 us -> 16.4 us (level)
  local copies, waits for them, and re-layouts: 0.68 us -> 0 us
  waiting for transfers between devices: 0.08 us -> 0.76 us
    ppermute x1, waiting for transfers between devices: 0.08 us -> 0.76 us  [paired(): mine = lax.ppermute(other, 'col', [(0, 1), (1, 0)])]
    unnamed x2 -> x0, local copies, waits for them, and re-layouts: 0.68 us -> none
where the time goes in v4:
time: 16.4 us; the launch traced here: 16.2 us
  blocking collectives  12.4 us (76%)
  Pallas kernels  2.19 us (13%)
  starting transfers between devices  0.86 us (5%)
  waiting for transfers between devices  0.76 us (5%)
    all_to_all x1, blocking collectives, paired(): lax.all_to_all(packed.reshape(groups * pitch, 1, width), ('row', 'col'),...  12.4 us
    pallas_call x1, Pallas kernels, paired(): pl.pallas_call(lambda *refs: pack_kernel(order, *refs), out_shape=[jax.Sh...  1.03 us
    ppermute x1, starting transfers between devices, paired(): mine = lax.ppermute(other, 'col', [(0, 1), (1, 0)])  0.86 us
    ppermute x1, waiting for transfers between devices, paired(): mine = lax.ppermute(other, 'col', [(0, 1), (1, 0)])  0.76 us
    pallas_call x1, Pallas kernels, paired(): pl.pallas_call(lambda *refs: last_kernel(pieces, *refs), out_shape=partia...  0.69 us
  transfers between devices with their start and end apart: 1, of which 1 were waited for; matrix products, arithmetic and copies ran while one was open for 0% of the time, Pallas kernels for 1%

profile of v4, /device:TPU:0, one launch (start us, length us, event | category | flops | bytes accessed | tf_op | source)
XLA Modules:
  0.0 16.2 jit_solution(11591448549692825448)
XLA Ops:
  0.0 1.0 %pack.1 = (f32[400,128]{1,0:T(8,128)S(1)}, f32[256,128]{1,0:T(8,128)S(1)}) custom-call(s32[2,16]{1,0:T(2,128)} %bitcast.14, s32[32,16]{1,0:T(8,128)} %bitcast.13, s32[1,256]{1,0:T(1,128)} %bitcast.15, f32[16,2,16,128]{3,2,1,0:T(8,128)} %bitcast.12), custom_call_target="tpu_custom_call" | custom-call | tf_op jit(solution)/shard_map/pack/pallas_call | solution.py:167
  1.0 12.4 %all_to_all.5 = f32[400,1,128]{2,1,0:T(1,128)S(1)} all-to-all(f32[400,1,128]{2,1,0:T(1,128)S(1)} %bitcast.11), channel_id=1, replica_groups={{23,17,10,6,27,29,8,4,31,25,14,19,21,2,12,0},{22,16,11,7,26,28,9,5,30,2..., dimensions={0} | all-to-all | bytes 409600 | tf_op jit(solution)/shard_map/all_to_all | solution.py:187
  13.4 0.2 %other_sums.1 = (f32[256,128]{1,0:T(8,128)S(1)}, bf16[384,256]{1,0:T(8,128)(2,1)S(1)}, s32[8,384]{1,0:T(8,128)S(1)}) custom-call(f32[400,128]{1,0:T(8,128)S(1)} %bitcast.10), custom_call_target="tpu_custom_call" | custom-call | tf_op jit(solution)/shard_map/other_sums/pallas_call | solution.py:195
  13.7 0.9 %collective-permute-start = (f32[256,128]{1,0:T(8,128)S(1)}, f32[256,128]{1,0:T(8,128)S(1)}, u32[]{:S(2)}, u32[]{:S(2)}) collective-permute-start(f32[256,128]{1,0:T(8,128)S(1)} %get-tuple-element.14), channel_id=1, source_target_pairs={{0,1},{1,0},{2,3},{3,2},{4,5},{5,4},{6,7},{7,6},{8,9},{9,8},{10,11... | collective-permute-start | bytes 393224 | tf_op jit(solution)/shard_map/ppermute | solution.py:207
  14.5 0.2 %own_sums.1.refs_0_ = f32[256,128]{1,0:T(8,128)S(1)} custom-call(bf16[384,256]{1,0:T(8,128)(2,1)S(1)} %get-tuple-element.11.refs_0_, s32[8,384]{1,0:T(8,128)S(1)} %get-tuple-element.12.refs_1_, f32[256,128]{1,0:T(8,128)S(1)} %get-tuple-element.13.refs_2_), custom_call_target="tpu_custom_call" | custom-call | flops 50331648 | bytes 1048576 | tf_op jit(solution)/shard_map/own_sums/pallas_call | solution.py:208
  14.7 0.8 %collective-permute-done.refs_1_ = f32[256,128]{1,0:T(8,128)S(1)} collective-permute-done((f32[256,128]{1,0:T(8,128)S(1)}, f32[256,128]{1,0:T(8,128)S(1)}, u32[]{:S(2)}, u32[]{:S(2)}) %collective-permute-start) | collective-permute-done | bytes 131104 | tf_op jit(solution)/shard_map/ppermute | solution.py:207
  15.5 0.7 %mean.1 = f32[256,128]{1,0:T(8,128)} custom-call(f32[256,128]{1,0:T(8,128)S(1)} %own_sums.1.refs_0_, f32[256,128]{1,0:T(8,128)S(1)} %collective-permute-done.refs_1_, f32[256,128]{1,0:T(8,128)S(1)} %get-tuple-element.13.refs_2_), custom_call_target="tpu_custom_call" | custom-call | tf_op jit(solution)/shard_map/mean/pallas_call | solution.py:218
Async XLA Ops:
  13.7 1.8 %collective-permute-start = (f32[256,128]{1,0:T(8,128)S(1)}, f32[256,128]{1,0:T(8,128)S(1)}, u32[]{:S(2)}, u32[]{:S(2)}) collective-permute-start(f32[256,128]{1,0:T(8,128)S(1)} %get-tuple-element.14), channel_id=1, source_target_pairs={{0,1},{1,0},{2,3},{3,2},{4,5},{5,4},{6,7},{7,6},{8,9},{9,8},{10,11... | collective-permute-start | bytes 393224 | tf_op jit(solution)/shard_map/ppermute | solution.py:207

commit v5 on v4

--- a/solution.py
+++ b/solution.py
@@ -7,7 +7,7 @@
 
 LANES = 128
 SUBLANES = 8
-FETCHES = 4
+FETCHES = 1
 SMALL = pltpu.CompilerParams(vmem_limit_bytes=8 << 20)
 
 
@@ -33,20 +33,28 @@
     return pltpu.with_memory_space_constraint(x, pltpu.HBM)
 
 
-ORDERS = {16: (11, 8, 5, 3, 13, 14, 4, 2, 15, 12, 7, 9, 10, 1, 6, 0)}
-
-
-def meeting_order(rows):
+TUNED = {
+    16: (
+        (
+            (11, 8, 5, 3, 9, 10, 4, 2, 15, 12, 7, 14, 6, 1, 13, 0),
+            (11, 8, 4, 5, 3, 6, 9, 2, 15, 12, 7, 14, 10, 1, 13, 0),
+        ),
+        (3, 8, 9, 10, 11, 12, 13, 14, 15),
+    ),
+}
+
+
+def exchange_plan(rows):
     first = rows * 3 // 4 - 1
-    return ORDERS.get(rows, (first, *(r for r in range(1, rows) if r != first), 0))
-
-
-def exchange_groups(order, cols):
-    swap = [int(2 * r >= len(order)) for r in order]
-    return [[r * cols + (c ^ s) for r, s in zip(order, swap)] for c in range(cols)]
-
-
-def pack_kernel(order, *refs):
+    order = (first, *(r for r in range(1, rows) if r != first), 0)
+    return TUNED.get(rows, ((order, order), tuple(range(rows // 2, rows))))
+
+
+def pick(index, values):
+    return sum(jnp.where(index == i, v, 0) for i, v in enumerate(values) if v)
+
+
+def pack_kernel(orders, swapped, *refs):
     counts_hbm, dst_hbm, degrees_hbm, messages_hbm, out_ref, share_ref = refs[:6]
     counts_ref, dst_ref, degrees_ref, messages_ref, sems = refs[6:]
     groups, _, slots, width = messages_ref.shape
@@ -65,7 +73,10 @@
     live = slots + half
     pitch = live + 1
     row = lax.axis_index("row")
-    place = sum(jnp.where(row == r, p, 0) for p, r in enumerate(order))
+    second_group = lax.axis_index("col") ^ pick(row, [int(r in swapped) for r in range(groups)])
+    places = [jnp.where(second_group == 1, orders[1].index(g), orders[0].index(g)) for g in range(groups)]
+    place = pick(row, [orders[0].index(r) for r in range(groups)])
+    place = jnp.where(second_group == 1, pick(row, [orders[1].index(r) for r in range(groups)]), place)
     lane = lax.broadcasted_iota(jnp.int32, (groups, width), 1)
     group = lax.broadcasted_iota(jnp.int32, (groups, width), 0)
     fill = jnp.zeros((groups, width - slots), jnp.int32)
@@ -83,25 +94,25 @@
     when_half = jnp.where(lane < half, first, by_half)
     labels = jnp.where(lane < live, jnp.where(full_rows == 1, when_full, when_half), 0)
     labels = pltpu.roll(labels.astype(jnp.float32), lax.rem(place * live, width), 1)
-    for p, g in enumerate(order):
-        out_ref[p * pitch + live : (p + 1) * pitch, :] = labels[g : g + 1, :]
+    for g in range(groups):
+        out_ref[pl.ds(places[g] * pitch + live, 1), :] = labels[g : g + 1, :]
     for start in range(0, owned, width):
         scale = jnp.maximum(degrees_ref[0:1, start : start + width], 1).astype(jnp.float32)
         share_ref[start : start + width, :] = jnp.transpose(jnp.broadcast_to(1.0 / scale, (width, width)))
     for g in range(groups):
         if g % size == 0:
             fetches[small + g // size].wait()
-        base = order.index(g) * pitch
+        base = places[g] * pitch
         a0 = messages_ref[g, 0, :half, :]
         a1 = messages_ref[g, 0, half:, :]
         b0 = messages_ref[g, 1, :half, :]
         b1 = messages_ref[g, 1, half:, :]
-        out_ref[base : base + half, :] = a0
-        out_ref[base + half : base + slots, :] = jnp.where(full[g], a1, b0)
-        out_ref[base + slots : base + live, :] = jnp.where(full[g], b0, b1)
-
-
-def slot_values(rows, received_ref, both_ref, label_ref):
+        out_ref[pl.ds(base, half), :] = a0
+        out_ref[pl.ds(base + half, half), :] = jnp.where(full[g], a1, b0)
+        out_ref[pl.ds(base + slots, half), :] = jnp.where(full[g], b0, b1)
+
+
+def slot_values(rows, received_ref):
     width = received_ref.shape[1]
     pitch = received_ref.shape[0] // rows
     live = pitch - 1
@@ -119,10 +130,7 @@
     values = jnp.concatenate([received_ref[p * pitch : p * pitch + live, :] for p in range(rows)], axis=0)
     high = values.astype(jnp.bfloat16)
     low = (values - high.astype(jnp.float32)).astype(jnp.bfloat16)
-    both = jnp.concatenate([high, low], axis=1)
-    both_ref[...] = both
-    label_ref[...] = jnp.broadcast_to(label, label_ref.shape)
-    return both, label
+    return jnp.concatenate([high, low], axis=1), label
 
 
 def range_sums(owned, side, both, label):
@@ -133,39 +141,27 @@
     return sums[:, :width] + sums[:, width:]
 
 
-def other_kernel(rows, owned, received_ref, other_ref, both_ref, label_ref):
-    both, label = slot_values(rows, received_ref, both_ref, label_ref)
-    other_ref[...] = range_sums(owned, 1 - lax.axis_index("col"), both, label)
-
-
-def own_kernel(owned, both_ref, label_ref, share_ref, own_ref):
-    sums = range_sums(owned, lax.axis_index("col"), both_ref[...], label_ref[0:1, :])
+def other_kernel(rows, owned, received_ref, other_ref):
+    other_ref[...] = range_sums(owned, 1 - lax.axis_index("col"), *slot_values(rows, received_ref))
+
+
+def own_kernel(rows, owned, received_ref, share_ref, own_ref):
+    sums = range_sums(owned, lax.axis_index("col"), *slot_values(rows, received_ref))
     own_ref[...] = sums * share_ref[...]
-
-
-def last_kernel(pieces, own_ref, mine_ref, share_ref, out_hbm, out_ref, sems):
-    size = out_ref.shape[0] // pieces
-    copies = []
-    for i in range(pieces):
-        piece = slice(i * size, (i + 1) * size)
-        out_ref[piece, :] = own_ref[piece, :] + mine_ref[piece, :] * share_ref[piece, :]
-        copies.append(pltpu.make_async_copy(out_ref.at[piece, :], out_hbm.at[piece, :], sems.at[i]))
-        copies[-1].start()
-    for copy in copies:
-        copy.wait()
 
 
 def paired(rows, messages, dst_local, counts, degrees):
     _, groups, subs, slots, width = messages.shape
     owned = degrees.shape[0]
     pitch = slots + slots // 2 + 1
-    order = meeting_order(rows)
+    orders, swapped = exchange_plan(rows)
+    members = [[r * subs + (c ^ int(r in swapped)) for r in order] for c, order in enumerate(orders)]
     total = rows * (pitch - 1)
     vmem = pl.BlockSpec(memory_space=pltpu.VMEM)
     hbm = pl.BlockSpec(memory_space=pltpu.HBM)
     partial = jax.ShapeDtypeStruct((owned, width), jnp.float32)
     packed, share = pl.pallas_call(
-        lambda *refs: pack_kernel(order, *refs),
+        lambda *refs: pack_kernel(orders, swapped, *refs),
         out_shape=[jax.ShapeDtypeStruct((groups * pitch, width), jnp.float32), partial],
         in_specs=[hbm] * 4,
         out_specs=[vmem] * 2,
@@ -190,40 +186,27 @@
         split_axis=0,
         concat_axis=0,
         tiled=True,
-        axis_index_groups=exchange_groups(order, 2),
+        axis_index_groups=members,
     ).reshape(groups * pitch, width)
-    other, both, label = pl.pallas_call(
+    other = pl.pallas_call(
         lambda *refs: other_kernel(rows, owned, *refs),
-        out_shape=[
-            partial,
-            jax.ShapeDtypeStruct((total, 2 * width), jnp.bfloat16),
-            jax.ShapeDtypeStruct((SUBLANES, total), jnp.int32),
-        ],
+        out_shape=partial,
         in_specs=[vmem],
-        out_specs=[vmem] * 3,
+        out_specs=vmem,
         compiler_params=SMALL,
         name="other_sums",
     )(received)
     mine = lax.ppermute(other, "col", [(0, 1), (1, 0)])
     own = pl.pallas_call(
-        lambda *refs: own_kernel(owned, *refs),
+        lambda *refs: own_kernel(rows, owned, *refs),
         out_shape=partial,
-        in_specs=[vmem] * 3,
+        in_specs=[vmem] * 2,
         out_specs=vmem,
         compiler_params=SMALL,
         cost_estimate=pl.CostEstimate(flops=4 * owned * total * width, bytes_accessed=1 << 20, transcendentals=0),
         name="own_sums",
-    )(both, label, share)
-    pieces = 4
-    return pl.pallas_call(
-        lambda *refs: last_kernel(pieces, *refs),
-        out_shape=partial,
-        in_specs=[vmem] * 3,
-        out_specs=hbm,
-        scratch_shapes=[pltpu.VMEM((owned, width), jnp.float32), pltpu.SemaphoreType.DMA((pieces,))],
-        compiler_params=SMALL,
-        name="mean",
-    )(own, mine, share)
+    )(received, share)
+    return own + mine * share
 
 
 def solution(mesh):

time: 16.4 us -> 16.2 us (0.988)
  other arithmetic: 0 us -> 0.68 us
  Pallas kernels: 2.19 us -> 1.52 us
  starting transfers between devices: 0.86 us -> 0.68 us
    add x0 -> x1, other arithmetic: none -> 0.68 us  [paired(): return own + mine * share]
    pallas_call x3 -> x2, Pallas kernels: 1.94 us -> 1.28 us  [the longest x1 1.04 us: paired(): pl.pallas_call(lambda *refs: pack_kernel(orders, swapped, *refs), out_sha...]
    ppermute x1, starting transfers between devices: 0.86 us -> 0.68 us  [paired(): mine = lax.ppermute(other, 'col', [(0, 1), (1, 0)])]
  transfers between devices with their start and end apart: 1 -> 1, of which waited for: 1 -> 1; matrix products, arithmetic and copies ran while one was open for 0% -> 0% of each run, Pallas kernels for 1% -> 2%
where the time goes in v5:
time: 16.2 us; the launch traced here: 16 us
  blocking collectives  12.3 us (76%)
  Pallas kernels  1.52 us (9%)
  waiting for transfers between devices  0.74 us (5%)
  starting transfers between devices  0.68 us (4%)
  other arithmetic  0.68 us (4%)
    all_to_all x1, blocking collectives, paired(): lax.all_to_all(packed.reshape(groups * pitch, 1, width), ('row', 'col'),...  12.3 us
    pallas_call x1, Pallas kernels, paired(): pl.pallas_call(lambda *refs: pack_kernel(orders, swapped, *refs), out_sha...  1.04 us
    ppermute x1, waiting for transfers between devices, paired(): mine = lax.ppermute(other, 'col', [(0, 1), (1, 0)])  0.74 us
    ppermute x1, starting transfers between devices, paired(): mine = lax.ppermute(other, 'col', [(0, 1), (1, 0)])  0.68 us
    add x1, other arithmetic, paired(): return own + mine * share  0.68 us
  transfers between devices with their start and end apart: 1, of which 1 were waited for; matrix products, arithmetic and copies ran while one was open for 0% of the time, Pallas kernels for 2%

profile of v5, /device:TPU:0, one launch (start us, length us, event | category | flops | bytes accessed | tf_op | source)
XLA Modules:
  0.0 16.0 jit_solution(4437556191782995242)
XLA Ops:
  0.0 1.0 %pack.1 = (f32[400,128]{1,0:T(8,128)S(1)}, f32[256,128]{1,0:T(8,128)S(1)}) custom-call(s32[2,16]{1,0:T(2,128)} %bitcast.15, s32[32,16]{1,0:T(8,128)} %bitcast.14, s32[1,256]{1,0:T(1,128)} %bitcast.16, f32[16,2,16,128]{3,2,1,0:T(8,128)} %bitcast.13), custom_call_target="tpu_custom_call" | custom-call | tf_op jit(solution)/shard_map/pack/pallas_call | solution.py:163
  1.0 12.3 %all_to_all.5 = f32[400,1,128]{2,1,0:T(1,128)S(1)} all-to-all(f32[400,1,128]{2,1,0:T(1,128)S(1)} %bitcast.12), channel_id=1, replica_groups={{23,17,10,7,19,21,8,4,31,25,14,29,12,2,27,0},{22,16,9,11,6,13,18,5,30,2..., dimensions={0} | all-to-all | bytes 409600 | tf_op jit(solution)/shard_map/all_to_all | solution.py:183
  13.4 0.2 %other_sums.1 = f32[256,128]{1,0:T(8,128)S(1)} custom-call(f32[400,128]{1,0:T(8,128)S(1)} %bitcast.10), custom_call_target="tpu_custom_call" | custom-call | tf_op jit(solution)/shard_map/other_sums/pallas_call | solution.py:191
  13.6 0.7 %collective-permute-start = (f32[256,128]{1,0:T(8,128)S(1)}, f32[256,128]{1,0:T(8,128)S(1)}, u32[]{:S(2)}, u32[]{:S(2)}) collective-permute-start(f32[256,128]{1,0:T(8,128)S(1)} %other_sums.1), channel_id=1, source_target_pairs={{0,1},{1,0},{2,3},{3,2},{4,5},{5,4},{6,7},{7,6},{8,9},{9,8},{10,11... | collective-permute-start | bytes 393224 | tf_op jit(solution)/shard_map/ppermute | solution.py:199
  14.3 0.2 %own_sums.1 = f32[256,128]{1,0:T(8,128)S(1)} custom-call(f32[400,128]{1,0:T(8,128)S(1)} %bitcast.11, f32[256,128]{1,0:T(8,128)S(1)} %get-tuple-element.8.refs_1_), custom_call_target="tpu_custom_call" | custom-call | flops 50331648 | bytes 1048576 | tf_op jit(solution)/shard_map/own_sums/pallas_call | solution.py:200
  14.5 0.7 %collective-permute-done = f32[256,128]{1,0:T(8,128)S(1)} collective-permute-done((f32[256,128]{1,0:T(8,128)S(1)}, f32[256,128]{1,0:T(8,128)S(1)}, u32[]{:S(2)}, u32[]{:S(2)}) %collective-permute-start) | collective-permute-done | bytes 131104 | tf_op jit(solution)/shard_map/ppermute | solution.py:199
  15.3 0.7 %multiply_add_fusion = f32[256,128]{1,0:T(8,128)} fusion(f32[256,128]{1,0:T(8,128)S(1)} %own_sums.1, f32[256,128]{1,0:T(8,128)S(1)} %collective-permute-done, f32[256,128]{1,0:T(8,128)S(1)} %get-tuple-element.8.refs_1_), kind=kLoop, calls=%fused_computation | loop fusion | flops 65536 | bytes 524288 | tf_op jit(solution)/shard_map/add | solution.py:209
Async XLA Ops:
  13.6 1.7 %collective-permute-start = (f32[256,128]{1,0:T(8,128)S(1)}, f32[256,128]{1,0:T(8,128)S(1)}, u32[]{:S(2)}, u32[]{:S(2)}) collective-permute-start(f32[256,128]{1,0:T(8,128)S(1)} %other_sums.1), channel_id=1, source_target_pairs={{0,1},{1,0},{2,3},{3,2},{4,5},{5,4},{6,7},{7,6},{8,9},{9,8},{10,11... | collective-permute-start | bytes 393224 | tf_op jit(solution)/shard_map/ppermute | solution.py:199

commit v6 on v5

--- a/solution.py
+++ b/solution.py
@@ -35,11 +35,8 @@
 
 TUNED = {
     16: (
-        (
-            (11, 8, 5, 3, 9, 10, 4, 2, 15, 12, 7, 14, 6, 1, 13, 0),
-            (11, 8, 4, 5, 3, 6, 9, 2, 15, 12, 7, 14, 10, 1, 13, 0),
-        ),
-        (3, 8, 9, 10, 11, 12, 13, 14, 15),
+        (11, 8, 5, 3, 9, 10, 4, 2, 15, 12, 7, 14, 6, 1, 13, 0),
+        (11, 2, 5, 3, 4, 6, 9, 8, 15, 12, 7, 14, 10, 1, 13, 0),
     ),
 }
 
@@ -47,7 +44,7 @@
 def exchange_plan(rows):
     first = rows * 3 // 4 - 1
     order = (first, *(r for r in range(1, rows) if r != first), 0)
-    return TUNED.get(rows, ((order, order), tuple(range(rows // 2, rows))))
+    return TUNED.get(rows, (order, order)), range(rows // 2, rows)
 
 
 def pick(index, values):

time: 16.2 us -> 16.2 us (level)
  no operation moved by 1% of the time
where the time goes in v6:
time: 16.2 us; the launch traced here: 16 us
  blocking collectives  12.3 us (76%)
  Pallas kernels  1.52 us (9%)
  waiting for transfers between devices  0.74 us (5%)
  starting transfers between devices  0.69 us (4%)
  other arithmetic  0.68 us (4%)
    all_to_all x1, blocking collectives, paired(): lax.all_to_all(packed.reshape(groups * pitch, 1, width), ('row', 'col'),...  12.3 us
    pallas_call x1, Pallas kernels, paired(): pl.pallas_call(lambda *refs: pack_kernel(orders, swapped, *refs), out_sha...  1.04 us
    ppermute x1, waiting for transfers between devices, paired(): mine = lax.ppermute(other, 'col', [(0, 1), (1, 0)])  0.74 us
    ppermute x1, starting transfers between devices, paired(): mine = lax.ppermute(other, 'col', [(0, 1), (1, 0)])  0.69 us
    add x1, other arithmetic, paired(): return own + mine * share  0.68 us
  transfers between devices with their start and end apart: 1, of which 1 were waited for; matrix products, arithmetic and copies ran while one was open for 0% of the time, Pallas kernels for 2%

profile of v6, /device:TPU:0, one launch (start us, length us, event | category | flops | bytes accessed | tf_op | source)
XLA Modules:
  0.0 16.0 jit_solution(14765978894509874049)
XLA Ops:
  0.0 1.0 %pack.1 = (f32[400,128]{1,0:T(8,128)S(1)}, f32[256,128]{1,0:T(8,128)S(1)}) custom-call(s32[2,16]{1,0:T(2,128)} %bitcast.15, s32[32,16]{1,0:T(8,128)} %bitcast.14, s32[1,256]{1,0:T(1,128)} %bitcast.16, f32[16,2,16,128]{3,2,1,0:T(8,128)} %bitcast.13), custom_call_target="tpu_custom_call" | custom-call | tf_op jit(solution)/shard_map/pack/pallas_call | solution.py:160
  1.0 12.3 %all_to_all.5 = f32[400,1,128]{2,1,0:T(1,128)S(1)} all-to-all(f32[400,1,128]{2,1,0:T(1,128)S(1)} %bitcast.12), channel_id=1, replica_groups={{23,17,10,6,19,21,8,4,31,25,14,29,12,2,27,0},{22,5,11,7,9,13,18,16,30,2..., dimensions={0} | all-to-all | bytes 409600 | tf_op jit(solution)/shard_map/all_to_all | solution.py:180
  13.4 0.2 %other_sums.1 = f32[256,128]{1,0:T(8,128)S(1)} custom-call(f32[400,128]{1,0:T(8,128)S(1)} %bitcast.10), custom_call_target="tpu_custom_call" | custom-call | tf_op jit(solution)/shard_map/other_sums/pallas_call | solution.py:188
  13.6 0.7 %collective-permute-start = (f32[256,128]{1,0:T(8,128)S(1)}, f32[256,128]{1,0:T(8,128)S(1)}, u32[]{:S(2)}, u32[]{:S(2)}) collective-permute-start(f32[256,128]{1,0:T(8,128)S(1)} %other_sums.1), channel_id=1, source_target_pairs={{0,1},{1,0},{2,3},{3,2},{4,5},{5,4},{6,7},{7,6},{8,9},{9,8},{10,11... | collective-permute-start | bytes 393224 | tf_op jit(solution)/shard_map/ppermute | solution.py:196
  14.3 0.2 %own_sums.1 = f32[256,128]{1,0:T(8,128)S(1)} custom-call(f32[400,128]{1,0:T(8,128)S(1)} %bitcast.11, f32[256,128]{1,0:T(8,128)S(1)} %get-tuple-element.8.refs_1_), custom_call_target="tpu_custom_call" | custom-call | flops 50331648 | bytes 1048576 | tf_op jit(solution)/shard_map/own_sums/pallas_call | solution.py:197
  14.5 0.7 %collective-permute-done = f32[256,128]{1,0:T(8,128)S(1)} collective-permute-done((f32[256,128]{1,0:T(8,128)S(1)}, f32[256,128]{1,0:T(8,128)S(1)}, u32[]{:S(2)}, u32[]{:S(2)}) %collective-permute-start) | collective-permute-done | bytes 131104 | tf_op jit(solution)/shard_map/ppermute | solution.py:196
  15.3 0.7 %multiply_add_fusion = f32[256,128]{1,0:T(8,128)} fusion(f32[256,128]{1,0:T(8,128)S(1)} %own_sums.1, f32[256,128]{1,0:T(8,128)S(1)} %collective-permute-done, f32[256,128]{1,0:T(8,128)S(1)} %get-tuple-element.8.refs_1_), kind=kLoop, calls=%fused_computation | loop fusion | flops 65536 | bytes 524288 | tf_op jit(solution)/shard_map/add | solution.py:206
Async XLA Ops:
  13.6 1.7 %collective-permute-start = (f32[256,128]{1,0:T(8,128)S(1)}, f32[256,128]{1,0:T(8,128)S(1)}, u32[]{:S(2)}, u32[]{:S(2)}) collective-permute-start(f32[256,128]{1,0:T(8,128)S(1)} %other_sums.1), channel_id=1, source_target_pairs={{0,1},{1,0},{2,3},{3,2},{4,5},{5,4},{6,7},{7,6},{8,9},{9,8},{10,11... | collective-permute-start | bytes 393224 | tf_op jit(solution)/shard_map/ppermute | solution.py:196

commit v7 on v6

--- a/solution.py
+++ b/solution.py
@@ -138,13 +138,27 @@
     return sums[:, :width] + sums[:, width:]
 
 
-def other_kernel(rows, owned, received_ref, other_ref):
-    other_ref[...] = range_sums(owned, 1 - lax.axis_index("col"), *slot_values(rows, received_ref))
-
-
 def own_kernel(rows, owned, received_ref, share_ref, own_ref):
     sums = range_sums(owned, lax.axis_index("col"), *slot_values(rows, received_ref))
     own_ref[...] = sums * share_ref[...]
+
+
+def last_kernel(rows, owned, received_ref, own_ref, share_ref, out_hbm, out_ref, sems):
+    both, label = slot_values(rows, received_ref)
+    width = out_ref.shape[1]
+    parts = sems.shape[0]
+    size = owned // parts
+    copies = []
+    for i in range(parts):
+        part = pl.ds(i * size, size)
+        vertex = lax.broadcasted_iota(jnp.int32, (size, both.shape[0]), 0) + i * size
+        hot = (vertex == label - lax.axis_index("col") * owned).astype(jnp.float32).astype(jnp.bfloat16)
+        sums = jnp.dot(hot, both, preferred_element_type=jnp.float32)
+        out_ref[part, :] = own_ref[part, :] + (sums[:, :width] + sums[:, width:]) * share_ref[part, :]
+        copies.append(pltpu.make_async_copy(out_ref.at[part, :], out_hbm.at[part, :], sems.at[i]))
+        copies[-1].start()
+    for copy in copies:
+        copy.wait()
 
 
 def paired(rows, messages, dst_local, counts, degrees):
@@ -185,15 +199,7 @@
         tiled=True,
         axis_index_groups=members,
     ).reshape(groups * pitch, width)
-    other = pl.pallas_call(
-        lambda *refs: other_kernel(rows, owned, *refs),
-        out_shape=partial,
-        in_specs=[vmem],
-        out_specs=vmem,
-        compiler_params=SMALL,
-        name="other_sums",
-    )(received)
-    mine = lax.ppermute(other, "col", [(0, 1), (1, 0)])
+    crossed = lax.ppermute(received, "col", [(0, 1), (1, 0)])
     own = pl.pallas_call(
         lambda *refs: own_kernel(rows, owned, *refs),
         out_shape=partial,
@@ -203,7 +209,16 @@
         cost_estimate=pl.CostEstimate(flops=4 * owned * total * width, bytes_accessed=1 << 20, transcendentals=0),
         name="own_sums",
     )(received, share)
-    return own + mine * share
+    parts = 2
+    return pl.pallas_call(
+        lambda *refs: last_kernel(rows, owned, *refs),
+        out_shape=partial,
+        in_specs=[vmem] * 3,
+        out_specs=hbm,
+        scratch_shapes=[pltpu.VMEM((owned, width), jnp.float32), pltpu.SemaphoreType.DMA((parts,))],
+        compiler_params=SMALL,
+        name="last_sums",
+    )(crossed, own, share)
 
 
 def solution(mesh):

time: 16.2 us -> 16.2 us (level)
  other arithmetic: 0.68 us -> 0 us
  Pallas kernels: 1.52 us -> 2.19 us
    add x1 -> x0, other arithmetic: 0.68 us -> none  [paired(): return own + mine * share]
    pallas_call x1, Pallas kernels: 0.24 us -> 0.91 us  [paired(): pl.pallas_call(lambda *refs: last_kernel(rows, owned, *refs), out_shape=p...]
where the time goes in v7:
time: 16.2 us; the launch traced here: 16 us
  blocking collectives  12.3 us (76%)
  Pallas kernels  2.19 us (14%)
  waiting for transfers between devices  0.83 us (5%)
  starting transfers between devices  0.62 us (4%)
    all_to_all x1, blocking collectives, paired(): lax.all_to_all(packed.reshape(groups * pitch, 1, width), ('row', 'col'),...  12.3 us
    pallas_call x1, Pallas kernels, paired(): pl.pallas_call(lambda *refs: pack_kernel(orders, swapped, *refs), out_sha...  1.04 us
    pallas_call x1, Pallas kernels, paired(): pl.pallas_call(lambda *refs: last_kernel(rows, owned, *refs), out_shape=p...  0.91 us
    ppermute x1, waiting for transfers between devices, paired(): crossed = lax.ppermute(received, 'col', [(0, 1), (1, 0)])  0.83 us
    ppermute x1, starting transfers between devices, paired(): crossed = lax.ppermute(received, 'col', [(0, 1), (1, 0)])  0.62 us
  transfers between devices with their start and end apart: 1, of which 1 were waited for; matrix products, arithmetic and copies ran while one was open for 0% of the time, Pallas kernels for 2%

profile of v7, /device:TPU:0, one launch (start us, length us, event | category | flops | bytes accessed | tf_op | source)
XLA Modules:
  0.0 16.0 jit_solution(10409376307056668386)
XLA Ops:
  0.0 1.0 %pack.1 = (f32[400,128]{1,0:T(8,128)S(1)}, f32[256,128]{1,0:T(8,128)S(1)}) custom-call(s32[2,16]{1,0:T(2,128)} %bitcast.15, s32[32,16]{1,0:T(8,128)} %bitcast.14, s32[1,256]{1,0:T(1,128)} %bitcast.16, f32[16,2,16,128]{3,2,1,0:T(8,128)} %bitcast.13), custom_call_target="tpu_custom_call" | custom-call | tf_op jit(solution)/shard_map/pack/pallas_call | solution.py:174
  1.0 12.3 %all_to_all.5 = f32[400,1,128]{2,1,0:T(1,128)S(1)} all-to-all(f32[400,1,128]{2,1,0:T(1,128)S(1)} %bitcast.12), channel_id=1, replica_groups={{23,17,10,6,19,21,8,4,31,25,14,29,12,2,27,0},{22,5,11,7,9,13,18,16,30,2..., dimensions={0} | all-to-all | bytes 409600 | tf_op jit(solution)/shard_map/all_to_all | solution.py:194
  13.4 0.6 %collective-permute-start = (f32[400,128]{1,0:T(8,128)S(1)}, f32[400,128]{1,0:T(8,128)S(1)}, u32[]{:S(2)}, u32[]{:S(2)}) collective-permute-start(f32[400,128]{1,0:T(8,128)S(1)} %bitcast.10), channel_id=1, source_target_pairs={{0,1},{1,0},{2,3},{3,2},{4,5},{5,4},{6,7},{7,6},{8,9},{9,8},{10,11... | collective-permute-start | bytes 614408 | tf_op jit(solution)/shard_map/ppermute | solution.py:202
  14.0 0.2 %own_sums.1.refs_1_ = f32[256,128]{1,0:T(8,128)S(1)} custom-call(f32[400,128]{1,0:T(8,128)S(1)} %bitcast.11, f32[256,128]{1,0:T(8,128)S(1)} %get-tuple-element.8.refs_1_.refs_2_), custom_call_target="tpu_custom_call" | custom-call | flops 50331648 | bytes 1048576 | tf_op jit(solution)/shard_map/own_sums/pallas_call | solution.py:203
  14.2 0.8 %collective-permute-done.refs_0_ = f32[400,128]{1,0:T(8,128)S(1)} collective-permute-done((f32[400,128]{1,0:T(8,128)S(1)}, f32[400,128]{1,0:T(8,128)S(1)}, u32[]{:S(2)}, u32[]{:S(2)}) %collective-permute-start) | collective-permute-done | bytes 204832 | tf_op jit(solution)/shard_map/ppermute | solution.py:202
  15.1 0.9 %last_sums.1 = f32[256,128]{1,0:T(8,128)} custom-call(f32[400,128]{1,0:T(8,128)S(1)} %collective-permute-done.refs_0_, f32[256,128]{1,0:T(8,128)S(1)} %own_sums.1.refs_1_, f32[256,128]{1,0:T(8,128)S(1)} %get-tuple-element.8.refs_1_.refs_2_), custom_call_target="tpu_custom_call" | custom-call | tf_op jit(solution)/shard_map/last_sums/pallas_call | solution.py:213
Async XLA Ops:
  13.4 1.7 %collective-permute-start = (f32[400,128]{1,0:T(8,128)S(1)}, f32[400,128]{1,0:T(8,128)S(1)}, u32[]{:S(2)}, u32[]{:S(2)}) collective-permute-start(f32[400,128]{1,0:T(8,128)S(1)} %bitcast.10), channel_id=1, source_target_pairs={{0,1},{1,0},{2,3},{3,2},{4,5},{5,4},{6,7},{7,6},{8,9},{9,8},{10,11... | collective-permute-start | bytes 614408 | tf_op jit(solution)/shard_map/ppermute | solution.py:202

commit v8 on v6

--- a/solution.py
+++ b/solution.py
@@ -90,7 +90,7 @@
     when_full = jnp.where(lane < slots, first, by_full)
     when_half = jnp.where(lane < half, first, by_half)
     labels = jnp.where(lane < live, jnp.where(full_rows == 1, when_full, when_half), 0)
-    labels = pltpu.roll(labels.astype(jnp.float32), lax.rem(place * live, width), 1)
+    labels = pltpu.roll(labels.astype(jnp.float32), lax.rem(place * slots, width), 1)
     for g in range(groups):
         out_ref[pl.ds(places[g] * pitch + live, 1), :] = labels[g : g + 1, :]
     for start in range(0, owned, width):
@@ -109,22 +109,25 @@
         out_ref[pl.ds(base + slots, half), :] = jnp.where(full[g], b0, b1)
 
 
-def slot_values(rows, received_ref):
+def slot_values(rows, side, received_ref):
     width = received_ref.shape[1]
     pitch = received_ref.shape[0] // rows
     live = pitch - 1
-    total = rows * live
+    half = live // 3
+    window = 2 * half
     labels = received_ref[pl.ds(live, rows, stride=pitch), :].astype(jnp.int32)
+    labels = pltpu.roll(labels, jnp.where(side == 1, width - half, 0), 1)
     place = lax.broadcasted_iota(jnp.int32, (rows, width), 0)
     lane = lax.broadcasted_iota(jnp.int32, (rows, width), 1)
-    slot = lax.rem(lane - lax.rem(place * live, width) + width, width)
-    position = place * live + slot
+    position = place * window + lax.rem(lane - lax.rem(place * window, width) + width, width)
+    inside = position < (place + 1) * window
     parts = []
-    for block in range(total // width):
-        inside = (slot < live) & (position >= block * width) & (position < (block + 1) * width)
-        parts.append(jnp.sum(jnp.where(inside, labels, 0), axis=0, keepdims=True))
+    for block in range(rows * window // width):
+        here = inside & (position >= block * width) & (position < (block + 1) * width)
+        parts.append(jnp.sum(jnp.where(here, labels, 0), axis=0, keepdims=True))
     label = jnp.concatenate(parts, axis=1)
-    values = jnp.concatenate([received_ref[p * pitch : p * pitch + live, :] for p in range(rows)], axis=0)
+    first = side * half
+    values = jnp.concatenate([received_ref[pl.ds(p * pitch + first, window), :] for p in range(rows)], axis=0)
     high = values.astype(jnp.bfloat16)
     low = (values - high.astype(jnp.float32)).astype(jnp.bfloat16)
     return jnp.concatenate([high, low], axis=1), label
@@ -138,12 +141,16 @@
     return sums[:, :width] + sums[:, width:]
 
 
+def side_sums(rows, owned, side, received_ref):
+    return range_sums(owned, side, *slot_values(rows, side, received_ref))
+
+
 def other_kernel(rows, owned, received_ref, other_ref):
-    other_ref[...] = range_sums(owned, 1 - lax.axis_index("col"), *slot_values(rows, received_ref))
+    other_ref[...] = side_sums(rows, owned, 1 - lax.axis_index("col"), received_ref)
 
 
 def own_kernel(rows, owned, received_ref, share_ref, own_ref):
-    sums = range_sums(owned, lax.axis_index("col"), *slot_values(rows, received_ref))
+    sums = side_sums(rows, owned, lax.axis_index("col"), received_ref)
     own_ref[...] = sums * share_ref[...]
 
 
@@ -153,7 +160,7 @@
     pitch = slots + slots // 2 + 1
     orders, swapped = exchange_plan(rows)
     members = [[r * subs + (c ^ int(r in swapped)) for r in order] for c, order in enumerate(orders)]
-    total = rows * (pitch - 1)
+    total = rows * slots
     vmem = pl.BlockSpec(memory_space=pltpu.VMEM)
     hbm = pl.BlockSpec(memory_space=pltpu.HBM)
     partial = jax.ShapeDtypeStruct((owned, width), jnp.float32)
@@ -211,8 +218,7 @@
 
     def body(messages, dst_local, counts, degrees):
         subs, slots, width = messages.shape[2:]
-        live = slots + slots // 2
-        fits = width == LANES and slots % (2 * SUBLANES) == 0 and rows * live % width == 0
+        fits = width == LANES and slots % (2 * SUBLANES) == 0 and rows * slots % width == 0
         if subs == cols == 2 and fits and rows <= 16:
             return paired(rows, messages, dst_local, counts, degrees)
         return general(messages, dst_local, counts, degrees)

time: 16.2 us -> 16.2 us (level)
  no operation moved by 1% of the time
where the time goes in v8:
time: 16.2 us; the launch traced here: 16 us
  blocking collectives  12.3 us (76%)
  Pallas kernels  1.52 us (9%)
  waiting for transfers between devices  0.74 us (5%)
  starting transfers between devices  0.69 us (4%)
  other arithmetic  0.68 us (4%)
    all_to_all x1, blocking collectives, paired(): lax.all_to_all(packed.reshape(groups * pitch, 1, width), ('row', 'col'),...  12.3 us
    pallas_call x1, Pallas kernels, paired(): pl.pallas_call(lambda *refs: pack_kernel(orders, swapped, *refs), out_sha...  1.04 us
    ppermute x1, waiting for transfers between devices, paired(): mine = lax.ppermute(other, 'col', [(0, 1), (1, 0)])  0.74 us
    ppermute x1, starting transfers between devices, paired(): mine = lax.ppermute(other, 'col', [(0, 1), (1, 0)])  0.69 us
    add x1, other arithmetic, paired(): return own + mine * share  0.68 us
  transfers between devices with their start and end apart: 1, of which 1 were waited for; matrix products, arithmetic and copies ran while one was open for 0% of the time, Pallas kernels for 2%

profile of v8, /device:TPU:0, one launch (start us, length us, event | category | flops | bytes accessed | tf_op | source)
XLA Modules:
  0.0 16.0 jit_solution(18390937510006941065)
XLA Ops:
  0.0 1.0 %pack.1 = (f32[400,128]{1,0:T(8,128)S(1)}, f32[256,128]{1,0:T(8,128)S(1)}) custom-call(s32[2,16]{1,0:T(2,128)} %bitcast.15, s32[32,16]{1,0:T(8,128)} %bitcast.14, s32[1,256]{1,0:T(1,128)} %bitcast.16, f32[16,2,16,128]{3,2,1,0:T(8,128)} %bitcast.13), custom_call_target="tpu_custom_call" | custom-call | tf_op jit(solution)/shard_map/pack/pallas_call | solution.py:167
  1.0 12.3 %all_to_all.5 = f32[400,1,128]{2,1,0:T(1,128)S(1)} all-to-all(f32[400,1,128]{2,1,0:T(1,128)S(1)} %bitcast.12), channel_id=1, replica_groups={{23,17,10,6,19,21,8,4,31,25,14,29,12,2,27,0},{22,5,11,7,9,13,18,16,30,2..., dimensions={0} | all-to-all | bytes 409600 | tf_op jit(solution)/shard_map/all_to_all | solution.py:187
  13.4 0.2 %other_sums.1 = f32[256,128]{1,0:T(8,128)S(1)} custom-call(f32[400,128]{1,0:T(8,128)S(1)} %bitcast.10), custom_call_target="tpu_custom_call" | custom-call | tf_op jit(solution)/shard_map/other_sums/pallas_call | solution.py:195
  13.6 0.7 %collective-permute-start = (f32[256,128]{1,0:T(8,128)S(1)}, f32[256,128]{1,0:T(8,128)S(1)}, u32[]{:S(2)}, u32[]{:S(2)}) collective-permute-start(f32[256,128]{1,0:T(8,128)S(1)} %other_sums.1), channel_id=1, source_target_pairs={{0,1},{1,0},{2,3},{3,2},{4,5},{5,4},{6,7},{7,6},{8,9},{9,8},{10,11... | collective-permute-start | bytes 393224 | tf_op jit(solution)/shard_map/ppermute | solution.py:203
  14.3 0.2 %own_sums.1 = f32[256,128]{1,0:T(8,128)S(1)} custom-call(f32[400,128]{1,0:T(8,128)S(1)} %bitcast.11, f32[256,128]{1,0:T(8,128)S(1)} %get-tuple-element.8.refs_1_), custom_call_target="tpu_custom_call" | custom-call | flops 33554432 | bytes 1048576 | tf_op jit(solution)/shard_map/own_sums/pallas_call | solution.py:204
  14.6 0.7 %collective-permute-done = f32[256,128]{1,0:T(8,128)S(1)} collective-permute-done((f32[256,128]{1,0:T(8,128)S(1)}, f32[256,128]{1,0:T(8,128)S(1)}, u32[]{:S(2)}, u32[]{:S(2)}) %collective-permute-start) | collective-permute-done | bytes 131104 | tf_op jit(solution)/shard_map/ppermute | solution.py:203
  15.3 0.7 %multiply_add_fusion = f32[256,128]{1,0:T(8,128)} fusion(f32[256,128]{1,0:T(8,128)S(1)} %own_sums.1, f32[256,128]{1,0:T(8,128)S(1)} %collective-permute-done, f32[256,128]{1,0:T(8,128)S(1)} %get-tuple-element.8.refs_1_), kind=kLoop, calls=%fused_computation | loop fusion | flops 65536 | bytes 524288 | tf_op jit(solution)/shard_map/add | solution.py:213
Async XLA Ops:
  13.6 1.7 %collective-permute-start = (f32[256,128]{1,0:T(8,128)S(1)}, f32[256,128]{1,0:T(8,128)S(1)}, u32[]{:S(2)}, u32[]{:S(2)}) collective-permute-start(f32[256,128]{1,0:T(8,128)S(1)} %other_sums.1), channel_id=1, source_target_pairs={{0,1},{1,0},{2,3},{3,2},{4,5},{5,4},{6,7},{7,6},{8,9},{9,8},{10,11... | collective-permute-start | bytes 393224 | tf_op jit(solution)/shard_map/ppermute | solution.py:203
